TPU v7x, 256 devices: a 2x2x32 block of a 4x8x32 slice. The times are simulated.
256 devices in a mesh: grp: 4 (over x, y), ep: 64 (over z, core).
Axes of the slice: x: 2, y: 2, z: 32, core: 2. Of those that a mesh axis runs over, the one named last changes fastest.
The devices are a block of a 4x8x32 slice.
Arguments:
- expert_ids: int32 [16384, 8], P(('grp', 'ep')), parts along dimension 0, may hold values from 0 to 63, all different within a row; in each aligned block of 64 rows (0 to 63, 64 to 127, ...) at most 16 rows name the same one
- route_gates: float32 [16384, 8], P(('grp', 'ep')), parts along dimension 0, may hold values from 0.1 to 0.5
- routed_in: bfloat16 [16384, 8, 2048], P(('grp', 'ep')), parts along dimension 0, may hold values from -6 to 6
- down_weight: bfloat16 [64, 1024, 3584], P('ep'), may hold values from -0.1875 to 0.1875
- slot_offset: int32 [1], replicated, may hold values from 0 to 63
Outputs:
- combined: bfloat16 [16384, 3584], P(('grp', 'ep')), parts along dimension 0
There are 4 independent parts, one for each index of `grp`. A program takes and returns all parts, laid end to end along the dimension named above; an argument that names none is the same for every part. Nothing has to cross between parts.
Inputs may be any that keep to these rules, and one draw needn't show every extreme that they name: `expert_ids`: each row names 8 different experts. Among the tokens of one ep device, no expert is named by more than 16 tokens, a bound that some block reaches in some devices.
All inputs are finite; a program needn't handle non-finite values.
Results may differ from a plain program's by a relative error of at most 0.0057.
Values may be sent and summed in bfloat16 or wider, within the bound.
No kernel may reach another device: no remote copies, remote signals or barrier semaphores. Data moves between devices by JAX's collectives and lax.ppermute only.
A program may use at most 128 MiB of HBM per device.

v0:
```python
import jax
import jax.numpy as jnp
from jax import lax
from jax.experimental import pallas as pl
from jax.experimental.pallas import tpu as pltpu
from jax.sharding import PartitionSpec as P

CHAINS = 2
STEPS = (4, 6, 6)
PIECES = (1, 2, 2)
PARTS = 4
INTERPRET = False


def strictly_before(size):
    earlier = lax.broadcasted_iota(jnp.int32, (size, size), 0)
    return (earlier < lax.broadcasted_iota(jnp.int32, (size, size), 1)).astype(jnp.bfloat16)


def pack_kernel(
    target_ref,
    gate_ref,
    routed_ref,
    out_ref,
    raw_ref,
    hidden_ref,
    table_ref,
    packed_ref,
    arrive,
    leave,
    *,
    capacity,
    chosen,
):
    pairs = target_ref.shape[1]
    chips = table_ref.shape[0]
    half = routed_ref.shape[1] // 2
    rows = pairs // PARTS
    block = chips // PARTS
    reads = [
        pltpu.make_async_copy(
            routed_ref.at[pl.ds(i * rows, rows)], raw_ref.at[pl.ds(i * rows, rows)], arrive.at[i]
        )
        for i in range(PARTS)
    ]
    writes = [
        pltpu.make_async_copy(
            packed_ref.at[pl.ds(i * block, block)], out_ref.at[pl.ds(i * block, block)], leave.at[i]
        )
        for i in range(PARTS)
    ]
    for read in reads:
        read.start()
    target = target_ref[...]
    named = lax.broadcasted_iota(jnp.int32, (2 * chips, pairs), 0) == target
    earlier = jnp.dot(
        named.astype(jnp.bfloat16), strictly_before(pairs), preferred_element_type=jnp.float32
    )
    rank = jnp.sum(jnp.where(named, earlier, 0.0), axis=0, keepdims=True).astype(jnp.int32)
    slot = target * capacity + rank
    at_rank = (lax.broadcasted_iota(jnp.int32, (capacity, pairs), 0) == rank).astype(jnp.bfloat16)
    token = (lax.broadcasted_iota(jnp.int32, (1, pairs), 1) // chosen).astype(jnp.float32)
    gate = gate_ref[...]
    high = gate.astype(jnp.bfloat16).astype(jnp.float32)
    rest = gate - high
    middle = rest.astype(jnp.bfloat16).astype(jnp.float32)
    table_ref[...] = jnp.zeros(table_ref.shape, jnp.float32)
    for side in range(2):
        mine = 2 * lax.broadcasted_iota(jnp.int32, (chips, pairs), 0) + side == target
        for kind, value in enumerate((token, high, middle, rest - middle)):
            found = lax.dot_general(
                jnp.where(mine, value, 0.0).astype(jnp.bfloat16),
                at_rank,
                (((1,), (1,)), ((), ())),
                preferred_element_type=jnp.float32,
            )
            for copy in range(3) if kind == 0 else (kind - 1,):
                start = (2 * copy + side) * capacity
                table_ref[:, min(kind, 1), start : start + capacity] = found
    for i, read in enumerate(reads):
        read.wait()
        at = slice(i * rows, (i + 1) * rows)
        gate = raw_ref[at, :half].astype(jnp.float32)
        upper = raw_ref[at, half:].astype(jnp.float32)
        hidden_ref[at, :] = (gate / (1.0 + jnp.exp(-gate)) * upper).astype(jnp.bfloat16)
    slots = block * 2 * capacity
    for i, write in enumerate(writes):
        wanted = lax.broadcasted_iota(jnp.int32, (slots, pairs), 0) + i * slots
        picked = jnp.dot(
            (wanted == slot).astype(jnp.bfloat16),
            hidden_ref[...],
            preferred_element_type=jnp.float32,
        ).astype(jnp.bfloat16)
        for chip in range(block):
            for tile in range(half // 128):
                packed_ref[i * block + chip, tile * 2 * capacity : (tile + 1) * 2 * capacity, :] = (
                    picked[
                        chip * 2 * capacity : (chip + 1) * 2 * capacity,
                        tile * 128 : (tile + 1) * 128,
                    ]
                )
        packed_ref[i * block : (i + 1) * block, (half // 128) * 2 * capacity :, :] = table_ref[
            i * block : (i + 1) * block
        ].astype(jnp.bfloat16)
        write.start()
    for write in writes:
        write.wait()


def pack(target, gates, routed, chips, capacity, chosen):
    pairs, width = routed.shape
    tall = width // 256 * 2 * capacity + 8
    return pl.pallas_call(
        lambda *refs: pack_kernel(*refs, capacity=capacity, chosen=chosen),
        in_specs=[
            pl.BlockSpec(memory_space=pltpu.VMEM),
            pl.BlockSpec(memory_space=pltpu.VMEM),
            pl.BlockSpec(memory_space=pltpu.HBM),
        ],
        out_specs=pl.BlockSpec(memory_space=pltpu.HBM),
        out_shape=jax.ShapeDtypeStruct((chips, tall, 128), jnp.bfloat16),
        scratch_shapes=[
            pltpu.VMEM((pairs, width), jnp.bfloat16),
            pltpu.VMEM((pairs, width // 2), jnp.bfloat16),
            pltpu.VMEM((chips, 8, 128), jnp.float32),
            pltpu.VMEM((chips, tall, 128), jnp.bfloat16),
            pltpu.SemaphoreType.DMA((PARTS,)),
            pltpu.SemaphoreType.DMA((PARTS,)),
        ],
        compiler_params=pltpu.CompilerParams(vmem_limit_bytes=60 * 1024 * 1024),
        interpret=INTERPRET,
    )(target, gates, routed)


def expert_kernel(place_ref, *refs, count, capacity):
    packed = refs[:count]
    own_weight, other_weight, out_ref = refs[count:]
    tokens = out_ref.shape[1]
    core = place_ref[1]
    tiles = own_weight.shape[0] // 128

    def project(side, weight):
        blocks = [
            jnp.concatenate(
                [
                    p[0, pl.ds(pl.multiple_of((2 * t + side) * capacity, capacity), capacity), :]
                    for t in range(tiles)
                ],
                axis=1,
            )
            for p in packed
        ]
        rows = jnp.concatenate(blocks, axis=0)
        return jnp.dot(rows, weight[...], preferred_element_type=jnp.float32).astype(jnp.bfloat16)

    own = project(core, own_weight)
    other = project(1 - core, other_weight)
    lower = jnp.where(core == 0, own, other)
    upper = jnp.where(core == 0, other, own)
    lanes = 6 * capacity
    wanted = lax.broadcasted_iota(jnp.int32, (tokens, lanes), 0).astype(jnp.float32)
    for i, p in enumerate(packed):
        at = slice(i * capacity, (i + 1) * capacity)
        stacked = jnp.concatenate([lower[at], upper[at]] * 3, axis=0)
        table = p[0, tiles * 2 * capacity :, :].astype(jnp.float32)
        scale = jnp.where(table[0:1, :lanes] == wanted, table[1:2, :lanes], 0.0).astype(jnp.bfloat16)
        out_ref[i] = jnp.dot(scale, stacked, preferred_element_type=jnp.float32).astype(
            jnp.bfloat16
        )


def expert_call(place, packed, own_weight, other_weight, homes, tokens, capacity, part, parts):
    chips, tall, _ = packed.shape
    width, columns = own_weight.shape
    columns = columns // parts
    steps = 2 if parts == CHAINS else 1
    piece = columns // steps
    count = len(homes)

    def row_spec(home):
        return pl.BlockSpec(
            (1, tall, 128), lambda j, s: (lax.rem(s[0] + (home + chips), chips), 0, 0)
        )

    weight_spec = pl.BlockSpec((width, piece), lambda j, s: (0, part * steps + j))
    grid_spec = pltpu.PrefetchScalarGridSpec(
        num_scalar_prefetch=1,
        grid=(steps,),
        in_specs=[row_spec(h) for h in homes] + [weight_spec] * 2,
        out_specs=pl.BlockSpec((count, tokens, piece), lambda j, s: (0, 0, j)),
    )
    flops = 4 * count * capacity * width * columns
    return pl.pallas_call(
        lambda *refs: expert_kernel(*refs, count=count, capacity=capacity),
        grid_spec=grid_spec,
        out_shape=jax.ShapeDtypeStruct((count, tokens, columns), jnp.bfloat16),
        cost_estimate=pl.CostEstimate(
            flops=flops, bytes_accessed=4 * width * columns, transcendentals=0
        ),
        compiler_params=pltpu.CompilerParams(
            dimension_semantics=("arbitrary",), vmem_limit_bytes=48 * 1024 * 1024
        ),
        interpret=INTERPRET,
    )(place, *([packed] * count), own_weight, other_weight)


def add_kernel(left_ref, *refs):
    own, out_ref = refs[:-1], refs[-1]
    wide = out_ref.shape[1] // len(own)

    def some(i, carry):
        at = pl.ds(pl.multiple_of(i * 16, 16), 16)
        for n, right_ref in enumerate(own):
            to = slice(n * wide, (n + 1) * wide)
            total = left_ref[at, to].astype(jnp.float32) + right_ref[0, at].astype(jnp.float32)
            out_ref[at, to] = total.astype(jnp.bfloat16)
        return carry

    lax.fori_loop(0, out_ref.shape[0] // 16, some, 0)


def add_own(arrived, batches, place):
    whole = pl.BlockSpec(arrived.shape, lambda i: (0, 0))
    return pl.pallas_call(
        add_kernel,
        grid=(1,),
        in_specs=[whole]
        + [pl.BlockSpec((1,) + batch.shape[1:], lambda i: (place, 0, 0)) for batch in batches],
        out_specs=whole,
        out_shape=jax.ShapeDtypeStruct(arrived.shape, jnp.bfloat16),
        compiler_params=pltpu.CompilerParams(vmem_limit_bytes=4 * 1024 * 1024),
        interpret=INTERPRET,
    )(arrived, *batches)


def on_device(expert_ids, route_gates, routed_in, down_weight, slot_offset):
    experts = lax.axis_size("ep")
    chips = experts // 2
    tokens, chosen = expert_ids.shape
    pairs = tokens * chosen
    capacity = 2 * pairs // experts
    weight = down_weight[0]
    index = lax.axis_index("ep")
    place = jnp.stack([index // 2, lax.rem(index, 2)]).astype(jnp.int32)

    def shifted(value, distance):
        return lax.ppermute(
            value, "ep", [(i, (i + 2 * distance) % experts) for i in range(experts)]
        )

    target = jnp.mod(expert_ids - slot_offset[0], experts).reshape(1, pairs)
    packed = pack(
        target,
        route_gates.reshape(1, pairs),
        routed_in.reshape(pairs, routed_in.shape[2]),
        chips,
        capacity,
        chosen,
    )
    same_core = [[2 * z + c for z in range(chips)] for c in range(2)]
    other_weight = lax.ppermute(weight, "ep", [(i, i ^ 1) for i in range(experts)])
    packed = lax.all_to_all(
        packed,
        "ep",
        split_axis=0,
        concat_axis=0,
        axis_index_groups=same_core,
        tiled=True,
    )


    half = chips // 2
    sums = {}
    first = 0
    for count, pieces in zip(STEPS, PIECES):
        steps = range(first, first + count)
        first += count
        homes = [half - s for s in steps] + [s + 1 - half for s in steps]
        for c in range(CHAINS):
            batches = []
            for piece in range(pieces):
                batches.append(
                    expert_call(
                        place,
                        packed,
                        weight,
                        other_weight,
                        homes,
                        tokens,
                        capacity,
                        c * pieces + piece,
                        CHAINS * pieces,
                    )
                )
            for i, home in enumerate(homes):
                sums[home, c] = (batches, i)

    def own_sum(home, c):
        batches, i = sums[home, c]
        return jnp.concatenate([batch[i] for batch in batches], axis=1)

    def with_own(arrived, home, c):
        return add_own(arrived, *sums[home, c])

    ahead = [own_sum(half, c) for c in range(CHAINS)]
    behind = [own_sum(1 - half, c) for c in range(CHAINS)]
    for step in range(half):
        for c in range(CHAINS):
            ahead[c] = shifted(ahead[c], 1)
            if step < half - 1:
                behind[c] = shifted(behind[c], -1)
                ahead[c] = with_own(ahead[c], half - 1 - step, c)
            if step < half - 2:
                behind[c] = with_own(behind[c], step + 2 - half, c)
    return jnp.concatenate(
        [
            (
                ahead[c].astype(jnp.float32)
                + behind[c].astype(jnp.float32)
                + own_sum(0, c).astype(jnp.float32)
            ).astype(jnp.bfloat16)
            for c in range(CHAINS)
        ],
        axis=1,
    )


def solution(mesh):
    placed = (
        P(("grp", "ep"), None),
        P(("grp", "ep"), None),
        P(("grp", "ep"), None, None),
        P("ep", None, None),
        P(),
    )
    return jax.shard_map(
        on_device, mesh=mesh, in_specs=placed, out_specs=P(("grp", "ep"), None), check_vma=False
    )
```

profile of v0, /device:TPU:46, one launch (start us, length us, event | category | flops | bytes accessed | tf_op | source)
XLA Modules:
  0.0 437.3 jit_solution(160974232678334076)
XLA Ops:
  3.6 4.5 %shard_map.55 = bf16[32,264,128]{2,1,0:T(8,128)(2,1)} custom-call(s32[1,512]{1,0:T(1,128)} %reshape.9.refs_0_, f32[1,512]{1,0:T(1,128)} %reshape.10.refs_1_, bf16[512,2048]{1,0:T(8,128)(2,1)} %bitcast.33), custom_call_target="tpu_custom_call" | custom-call | tf_op jit(solution)/shard_map/pallas_call | solution.py:113
  8.0 32.7 %all-to-all-start = ((bf16[32,264,128]{2,1,0:T(8,128)(2,1)}), bf16[32,264,128]{2,1,0:T(8,128)(2,1)S(1)}, u32[]{:S(2)}, u32[]{:S(2)}) async-start(bf16[32,264,128]{2,1,0:T(8,128)(2,1)} %shard_map.55), calls=%async_computation | async-start | bytes 4325376 | tf_op jit(solution)/shard_map/all_to_all | solution.py:262
  41.0 11.9 %collective-permute-done.refs_10_.refs_14_ = bf16[1024,3584]{1,0:T(8,128)(2,1)} collective-permute-done((bf16[1024,3584]{1,0:T(8,128)(2,1)}, bf16[1024,3584]{1,0:T(8,128)(2,1)}, u32[]{:S(2)}, u32[]{:S(2)}) %collective-permute-start) | collective-permute-done | bytes 7340064 | tf_op jit(solution)/shard_map/ppermute | solution.py:261
  52.8 189.7 %all-to-all-done.refs_1_.refs_2_.refs_3_.refs_4_.refs_5_.refs_6_.refs_7_.refs_8_.refs_9_.refs_10_.refs_11_.refs_12_ = bf16[32,264,128]{2,1,0:T(8,128)(2,1)S(1)} async-done(((bf16[32,264,128]{2,1,0:T(8,128)(2,1)}), bf16[32,264,128]{2,1,0:T(8,128)(2,1)S(1)}, u32[]{:S(2)}, u32[]{:S(2)}) %all-to-all-start) | async-done | bytes 2162720 | tf_op jit(solution)/shard_map/all_to_all | solution.py:262
  242.6 5.0 %shard_map.56.refs_0_ = bf16[8,64,1792]{2,1,0:T(8,128)(2,1)S(1)} custom-call(s32[2]{0:T(128)S(1)} %pad_add_fusion.refs_0_, bf16[32,264,128]{2,1,0:T(8,128)(2,1)S(1)} %all-to-all-done.refs_1_.refs_2_.refs_3_.refs_4_.refs_5_.refs_6_.refs_7_.refs_8_.refs_9_.refs_10_.refs_11_.refs_12_, ...), custom_call_target="tpu_custom_call" | custom-call | flops 939524096 | bytes 7340032 | tf_op jit(solution)/shard_map/pallas_call | solution.py:193
  247.7 3.2 collective-permute-start.17
  250.9 5.0 %shard_map.90.refs_0_ = bf16[8,64,1792]{2,1,0:T(8,128)(2,1)S(1)} custom-call(s32[2]{0:T(128)S(1)} %pad_add_fusion.refs_0_, bf16[32,264,128]{2,1,0:T(8,128)(2,1)S(1)} %all-to-all-done.refs_1_.refs_2_.refs_3_.refs_4_.refs_5_.refs_6_.refs_7_.refs_8_.refs_9_.refs_10_.refs_11_.refs_12_, ...), custom_call_target="tpu_custom_call" | custom-call | flops 939524096 | bytes 7340032 | tf_op jit(solution)/shard_map/pallas_call | solution.py:193
  256.3 3.3 collective-permute-start.48
  261.7 3.5 collective-permute-done.32.left_ref
  265.6 4.5 %collective-permute-done.2.left_ref = bf16[64,1792]{1,0:T(8,128)(2,1)S(1)} collective-permute-done((bf16[64,1792]{1,0:T(8,128)(2,1)S(1)}, bf16[64,1792]{1,0:T(8,128)(2,1)S(1)}, u32[]{:S(2)}, u32[]{:S(2)}) %collective-permute-start.2) | collective-permute-done | bytes 229408 | tf_op jit(solution)/shard_map/ppermute | solution.py:247
  270.4 3.3 collective-permute-start.49
  276.1 4.1 collective-permute-done.3.left_ref
  280.4 4.1 shard_map.60.refs_0_
  284.5 4.1 shard_map.61.refs_1_
  288.6 3.3 collective-permute-start.50
  292.3 2.1 collective-permute-start.35
  295.0 4.1 shard_map.94.refs_0_
  299.1 4.1 shard_map.95.refs_1_
  303.3 3.3 collective-permute-start.51
  309.2 3.3 collective-permute-done.51.left_ref
  312.7 3.8 collective-permute-start.52
  317.6 3.8 collective-permute-start.22
  321.9 3.4 collective-permute-start.53
  327.5 3.8 collective-permute-start.23
  331.5 2.9 collective-permute-done.7.left_ref
  334.9 3.3 collective-permute-start.54
  338.3 2.9 collective-permute-start.24
  341.4 2.8 collective-permute-done.8.left_ref
  344.5 3.3 collective-permute-start.55
  352.0 4.1 shard_map.68.refs_0_
  356.1 4.1 shard_map.69.refs_1_
  360.3 3.3 collective-permute-start.56
  363.9 2.1 collective-permute-start.41
  366.5 4.1 shard_map.102.refs_0_
  370.6 4.1 shard_map.103.refs_1_
  374.8 3.3 collective-permute-start.57
  380.7 3.3 collective-permute-done.57.left_ref
  384.1 3.8 collective-permute-start.58
  389.1 3.8 collective-permute-start.28
  394.0 3.8 collective-permute-start.59
  398.9 3.8 collective-permute-start.29
  408.9 3.7 collective-permute-start.30
  412.8 4.4 %collective-permute-done.14.left_ref = bf16[64,1792]{1,0:T(8,128)(2,1)S(1)} collective-permute-done((bf16[64,1792]{1,0:T(8,128)(2,1)S(1)}, bf16[64,1792]{1,0:T(8,128)(2,1)S(1)}, u32[]{:S(2)}, u32[]{:S(2)}) %collective-permute-start.14) | collective-permute-done | bytes 229408 | tf_op jit(solution)/shard_map/ppermute | solution.py:247
  417.6 3.3 collective-permute-start.61
  421.2 2.1 collective-permute-start.46
  425.0 3.3 collective-permute-start.62
  429.5 2.6 collective-permute-done.16
  432.2 3.8 collective-permute-done.47
  (162 shorter events, 39.8 us)
Async XLA Ops:
  8.0 234.5 %all-to-all-start = ((bf16[32,264,128]{2,1,0:T(8,128)(2,1)}), bf16[32,264,128]{2,1,0:T(8,128)(2,1)S(1)}, u32[]{:S(2)}, u32[]{:S(2)}) async-start(bf16[32,264,128]{2,1,0:T(8,128)(2,1)} %shard_map.55), calls=%async_computation | async-start | bytes 4325376 | tf_op jit(solution)/shard_map/all_to_all | solution.py:262
  40.7 12.1 %collective-permute-start = (bf16[1024,3584]{1,0:T(8,128)(2,1)}, bf16[1024,3584]{1,0:T(8,128)(2,1)}, u32[]{:S(2)}, u32[]{:S(2)}) collective-permute-start(bf16[1024,3584]{1,0:T(8,128)(2,1)} %bitcast.22), channel_id=1, source_target_pairs={{0,1},{1,0},{2,3},{3,2},{4,5},{5,4},{6,7},{7,6},{8,9},{9,8},{10,11... | collective-permute-start | bytes 22020104 | tf_op jit(solution)/shard_map/ppermute | solution.py:261
  247.7 11.9 %collective-permute-start.17 = (bf16[64,1792]{1,0:T(8,128)(2,1)S(1)}, bf16[64,1792]{1,0:T(8,128)(2,1)S(1)}, u32[]{:S(2)}, u32[]{:S(2)}) collective-permute-start(bf16[64,1792]{1,0:T(8,128)(2,1)S(1)} %get-tuple-element.6), channel_id=1, source_target_pairs={{0,62},{1,63},{2,0},{3,1},{4,2},{5,3},{6,4},{7,5},{8,6},{9,7},{10,... | collective-permute-start | bytes 688136 | tf_op jit(solution)/shard_map/ppermute | solution.py:247
  256.2 13.9 %collective-permute-start.2 = (bf16[64,1792]{1,0:T(8,128)(2,1)S(1)}, bf16[64,1792]{1,0:T(8,128)(2,1)S(1)}, u32[]{:S(2)}, u32[]{:S(2)}) collective-permute-start(bf16[64,1792]{1,0:T(8,128)(2,1)S(1)} %shard_map.57), channel_id=1, source_target_pairs={{0,2},{1,3},{2,4},{3,5},{4,6},{5,7},{6,8},{7,9},{8,10},{9,11},{10,... | collective-permute-start | bytes 688136 | tf_op jit(solution)/shard_map/ppermute | solution.py:247
  256.3 14.0 %collective-permute-start.48 = (bf16[64,1792]{1,0:T(8,128)(2,1)S(1)}, bf16[64,1792]{1,0:T(8,128)(2,1)S(1)}, u32[]{:S(2)}, u32[]{:S(2)}) collective-permute-start(bf16[64,1792]{1,0:T(8,128)(2,1)S(1)} %get-tuple-element.8), channel_id=1, source_target_pairs={{0,62},{1,63},{2,0},{3,1},{4,2},{5,3},{6,4},{7,5},{8,6},{9,7},{10,... | collective-permute-start | bytes 688136 | tf_op jit(solution)/shard_map/ppermute | solution.py:247
  259.7 14.0 %collective-permute-start.18 = (bf16[64,1792]{1,0:T(8,128)(2,1)S(1)}, bf16[64,1792]{1,0:T(8,128)(2,1)S(1)}, u32[]{:S(2)}, u32[]{:S(2)}) collective-permute-start(bf16[64,1792]{1,0:T(8,128)(2,1)S(1)} %shard_map.76), channel_id=1, source_target_pairs={{0,62},{1,63},{2,0},{3,1},{4,2},{5,3},{6,4},{7,5},{8,6},{9,7},{10,... | collective-permute-start | bytes 688136 | tf_op jit(solution)/shard_map/ppermute | solution.py:247
  265.2 10.0 %collective-permute-start.33 = (bf16[64,1792]{1,0:T(8,128)(2,1)S(1)}, bf16[64,1792]{1,0:T(8,128)(2,1)S(1)}, u32[]{:S(2)}, u32[]{:S(2)}) collective-permute-start(bf16[64,1792]{1,0:T(8,128)(2,1)S(1)} %shard_map.91), channel_id=1, source_target_pairs={{0,2},{1,3},{2,4},{3,5},{4,6},{5,7},{6,8},{7,9},{8,10},{9,11},{10,... | collective-permute-start | bytes 688136 | tf_op jit(solution)/shard_map/ppermute | solution.py:247
  270.1 10.0 %collective-permute-start.3 = (bf16[64,1792]{1,0:T(8,128)(2,1)S(1)}, bf16[64,1792]{1,0:T(8,128)(2,1)S(1)}, u32[]{:S(2)}, u32[]{:S(2)}) collective-permute-start(bf16[64,1792]{1,0:T(8,128)(2,1)S(1)} %shard_map.58), channel_id=1, source_target_pairs={{0,2},{1,3},{2,4},{3,5},{4,6},{5,7},{6,8},{7,9},{8,10},{9,11},{10,... | collective-permute-start | bytes 688136 | tf_op jit(solution)/shard_map/ppermute | solution.py:247
  270.4 18.2 %collective-permute-start.49 = (bf16[64,1792]{1,0:T(8,128)(2,1)S(1)}, bf16[64,1792]{1,0:T(8,128)(2,1)S(1)}, u32[]{:S(2)}, u32[]{:S(2)}) collective-permute-start(bf16[64,1792]{1,0:T(8,128)(2,1)S(1)} %shard_map.110), channel_id=1, source_target_pairs={{0,62},{1,63},{2,0},{3,1},{4,2},{5,3},{6,4},{7,5},{8,6},{9,7},{10,... | collective-permute-start | bytes 688136 | tf_op jit(solution)/shard_map/ppermute | solution.py:247
  273.8 18.2 %collective-permute-start.19 = (bf16[64,1792]{1,0:T(8,128)(2,1)S(1)}, bf16[64,1792]{1,0:T(8,128)(2,1)S(1)}, u32[]{:S(2)}, u32[]{:S(2)}) collective-permute-start(bf16[64,1792]{1,0:T(8,128)(2,1)S(1)} %shard_map.77), channel_id=1, source_target_pairs={{0,62},{1,63},{2,0},{3,1},{4,2},{5,3},{6,4},{7,5},{8,6},{9,7},{10,... | collective-permute-start | bytes 688136 | tf_op jit(solution)/shard_map/ppermute | solution.py:247
  275.3 16.9 %collective-permute-start.34 = (bf16[64,1792]{1,0:T(8,128)(2,1)S(1)}, bf16[64,1792]{1,0:T(8,128)(2,1)S(1)}, u32[]{:S(2)}, u32[]{:S(2)}) collective-permute-start(bf16[64,1792]{1,0:T(8,128)(2,1)S(1)} %shard_map.92), channel_id=1, source_target_pairs={{0,2},{1,3},{2,4},{3,5},{4,6},{5,7},{6,8},{7,9},{8,10},{9,11},{10,... | collective-permute-start | bytes 688136 | tf_op jit(solution)/shard_map/ppermute | solution.py:247
  280.2 14.1 %collective-permute-start.4 = (bf16[64,1792]{1,0:T(8,128)(2,1)S(1)}, bf16[64,1792]{1,0:T(8,128)(2,1)S(1)}, u32[]{:S(2)}, u32[]{:S(2)}) collective-permute-start(bf16[64,1792]{1,0:T(8,128)(2,1)S(1)} %shard_map.59), channel_id=1, source_target_pairs={{0,2},{1,3},{2,4},{3,5},{4,6},{5,7},{6,8},{7,9},{8,10},{9,11},{10,... | collective-permute-start | bytes 688136 | tf_op jit(solution)/shard_map/ppermute | solution.py:247
  288.6 14.5 %collective-permute-start.50 = (bf16[64,1792]{1,0:T(8,128)(2,1)S(1)}, bf16[64,1792]{1,0:T(8,128)(2,1)S(1)}, u32[]{:S(2)}, u32[]{:S(2)}) collective-permute-start(bf16[64,1792]{1,0:T(8,128)(2,1)S(1)} %shard_map.111), channel_id=1, source_target_pairs={{0,62},{1,63},{2,0},{3,1},{4,2},{5,3},{6,4},{7,5},{8,6},{9,7},{10,... | collective-permute-start | bytes 688136 | tf_op jit(solution)/shard_map/ppermute | solution.py:247
  292.0 14.6 %collective-permute-start.20 = (bf16[64,1792]{1,0:T(8,128)(2,1)S(1)}, bf16[64,1792]{1,0:T(8,128)(2,1)S(1)}, u32[]{:S(2)}, u32[]{:S(2)}) collective-permute-start(bf16[64,1792]{1,0:T(8,128)(2,1)S(1)} %shard_map.78), channel_id=1, source_target_pairs={{0,62},{1,63},{2,0},{3,1},{4,2},{5,3},{6,4},{7,5},{8,6},{9,7},{10,... | collective-permute-start | bytes 688136 | tf_op jit(solution)/shard_map/ppermute | solution.py:247
  292.3 14.6 %collective-permute-start.35 = (bf16[64,1792]{1,0:T(8,128)(2,1)S(1)}, bf16[64,1792]{1,0:T(8,128)(2,1)S(1)}, u32[]{:S(2)}, u32[]{:S(2)}) collective-permute-start(bf16[64,1792]{1,0:T(8,128)(2,1)S(1)} %shard_map.93), channel_id=1, source_target_pairs={{0,2},{1,3},{2,4},{3,5},{4,6},{5,7},{6,8},{7,9},{8,10},{9,11},{10,... | collective-permute-start | bytes 688136 | tf_op jit(solution)/shard_map/ppermute | solution.py:247
  294.5 14.6 %collective-permute-start.5 = (bf16[64,1792]{1,0:T(8,128)(2,1)S(1)}, bf16[64,1792]{1,0:T(8,128)(2,1)S(1)}, u32[]{:S(2)}, u32[]{:S(2)}) collective-permute-start(bf16[64,1792]{1,0:T(8,128)(2,1)S(1)} %shard_map.62), channel_id=1, source_target_pairs={{0,2},{1,3},{2,4},{3,5},{4,6},{5,7},{6,8},{7,9},{8,10},{9,11},{10,... | collective-permute-start | bytes 688136 | tf_op jit(solution)/shard_map/ppermute | solution.py:247
  306.7 10.8 %collective-permute-start.21 = (bf16[64,1792]{1,0:T(8,128)(2,1)S(1)}, bf16[64,1792]{1,0:T(8,128)(2,1)S(1)}, u32[]{:S(2)}, u32[]{:S(2)}) collective-permute-start(bf16[64,1792]{1,0:T(8,128)(2,1)S(1)} %shard_map.79), channel_id=1, source_target_pairs={{0,62},{1,63},{2,0},{3,1},{4,2},{5,3},{6,4},{7,5},{8,6},{9,7},{10,... | collective-permute-start | bytes 688136 | tf_op jit(solution)/shard_map/ppermute | solution.py:247
  306.9 14.5 %collective-permute-start.36 = (bf16[64,1792]{1,0:T(8,128)(2,1)S(1)}, bf16[64,1792]{1,0:T(8,128)(2,1)S(1)}, u32[]{:S(2)}, u32[]{:S(2)}) collective-permute-start(bf16[64,1792]{1,0:T(8,128)(2,1)S(1)} %shard_map.96), channel_id=1, source_target_pairs={{0,2},{1,3},{2,4},{3,5},{4,6},{5,7},{6,8},{7,9},{8,10},{9,11},{10,... | collective-permute-start | bytes 688136 | tf_op jit(solution)/shard_map/ppermute | solution.py:247
  309.1 12.5 %collective-permute-start.6 = (bf16[64,1792]{1,0:T(8,128)(2,1)S(1)}, bf16[64,1792]{1,0:T(8,128)(2,1)S(1)}, u32[]{:S(2)}, u32[]{:S(2)}) collective-permute-start(bf16[64,1792]{1,0:T(8,128)(2,1)S(1)} %shard_map.63), channel_id=1, source_target_pairs={{0,2},{1,3},{2,4},{3,5},{4,6},{5,7},{6,8},{7,9},{8,10},{9,11},{10,... | collective-permute-start | bytes 688136 | tf_op jit(solution)/shard_map/ppermute | solution.py:247
  317.6 9.8 %collective-permute-start.22 = (bf16[64,1792]{1,0:T(8,128)(2,1)S(1)}, bf16[64,1792]{1,0:T(8,128)(2,1)S(1)}, u32[]{:S(2)}, u32[]{:S(2)}) collective-permute-start(bf16[64,1792]{1,0:T(8,128)(2,1)S(1)} %shard_map.80), channel_id=1, source_target_pairs={{0,62},{1,63},{2,0},{3,1},{4,2},{5,3},{6,4},{7,5},{8,6},{9,7},{10,... | collective-permute-start | bytes 688136 | tf_op jit(solution)/shard_map/ppermute | solution.py:247
  321.5 9.8 %collective-permute-start.37 = (bf16[64,1792]{1,0:T(8,128)(2,1)S(1)}, bf16[64,1792]{1,0:T(8,128)(2,1)S(1)}, u32[]{:S(2)}, u32[]{:S(2)}) collective-permute-start(bf16[64,1792]{1,0:T(8,128)(2,1)S(1)} %shard_map.97), channel_id=1, source_target_pairs={{0,2},{1,3},{2,4},{3,5},{4,6},{5,7},{6,8},{7,9},{8,10},{9,11},{10,... | collective-permute-start | bytes 688136 | tf_op jit(solution)/shard_map/ppermute | solution.py:247
  321.7 12.7 %collective-permute-start.7 = (bf16[64,1792]{1,0:T(8,128)(2,1)S(1)}, bf16[64,1792]{1,0:T(8,128)(2,1)S(1)}, u32[]{:S(2)}, u32[]{:S(2)}) collective-permute-start(bf16[64,1792]{1,0:T(8,128)(2,1)S(1)} %shard_map.64), channel_id=1, source_target_pairs={{0,2},{1,3},{2,4},{3,5},{4,6},{5,7},{6,8},{7,9},{8,10},{9,11},{10,... | collective-permute-start | bytes 688136 | tf_op jit(solution)/shard_map/ppermute | solution.py:247
  321.9 12.8 %collective-permute-start.53 = (bf16[64,1792]{1,0:T(8,128)(2,1)S(1)}, bf16[64,1792]{1,0:T(8,128)(2,1)S(1)}, u32[]{:S(2)}, u32[]{:S(2)}) collective-permute-start(bf16[64,1792]{1,0:T(8,128)(2,1)S(1)} %shard_map.114), channel_id=1, source_target_pairs={{0,62},{1,63},{2,0},{3,1},{4,2},{5,3},{6,4},{7,5},{8,6},{9,7},{10,... | collective-permute-start | bytes 688136 | tf_op jit(solution)/shard_map/ppermute | solution.py:247
  327.5 10.7 %collective-permute-start.23 = (bf16[64,1792]{1,0:T(8,128)(2,1)S(1)}, bf16[64,1792]{1,0:T(8,128)(2,1)S(1)}, u32[]{:S(2)}, u32[]{:S(2)}) collective-permute-start(bf16[64,1792]{1,0:T(8,128)(2,1)S(1)} %shard_map.81), channel_id=1, source_target_pairs={{0,62},{1,63},{2,0},{3,1},{4,2},{5,3},{6,4},{7,5},{8,6},{9,7},{10,... | collective-permute-start | bytes 688136 | tf_op jit(solution)/shard_map/ppermute | solution.py:247
  331.3 9.8 %collective-permute-start.38 = (bf16[64,1792]{1,0:T(8,128)(2,1)S(1)}, bf16[64,1792]{1,0:T(8,128)(2,1)S(1)}, u32[]{:S(2)}, u32[]{:S(2)}) collective-permute-start(bf16[64,1792]{1,0:T(8,128)(2,1)S(1)} %shard_map.98), channel_id=1, source_target_pairs={{0,2},{1,3},{2,4},{3,5},{4,6},{5,7},{6,8},{7,9},{8,10},{9,11},{10,... | collective-permute-start | bytes 688136 | tf_op jit(solution)/shard_map/ppermute | solution.py:247
  334.5 9.7 %collective-permute-start.8 = (bf16[64,1792]{1,0:T(8,128)(2,1)S(1)}, bf16[64,1792]{1,0:T(8,128)(2,1)S(1)}, u32[]{:S(2)}, u32[]{:S(2)}) collective-permute-start(bf16[64,1792]{1,0:T(8,128)(2,1)S(1)} %shard_map.65), channel_id=1, source_target_pairs={{0,2},{1,3},{2,4},{3,5},{4,6},{5,7},{6,8},{7,9},{8,10},{9,11},{10,... | collective-permute-start | bytes 688136 | tf_op jit(solution)/shard_map/ppermute | solution.py:247
  338.3 9.5 %collective-permute-start.24 = (bf16[64,1792]{1,0:T(8,128)(2,1)S(1)}, bf16[64,1792]{1,0:T(8,128)(2,1)S(1)}, u32[]{:S(2)}, u32[]{:S(2)}) collective-permute-start(bf16[64,1792]{1,0:T(8,128)(2,1)S(1)} %shard_map.82), channel_id=1, source_target_pairs={{0,62},{1,63},{2,0},{3,1},{4,2},{5,3},{6,4},{7,5},{8,6},{9,7},{10,... | collective-permute-start | bytes 688136 | tf_op jit(solution)/shard_map/ppermute | solution.py:247
  344.5 15.7 %collective-permute-start.55 = (bf16[64,1792]{1,0:T(8,128)(2,1)S(1)}, bf16[64,1792]{1,0:T(8,128)(2,1)S(1)}, u32[]{:S(2)}, u32[]{:S(2)}) collective-permute-start(bf16[64,1792]{1,0:T(8,128)(2,1)S(1)} %shard_map.116), channel_id=1, source_target_pairs={{0,62},{1,63},{2,0},{3,1},{4,2},{5,3},{6,4},{7,5},{8,6},{9,7},{10,... | collective-permute-start | bytes 688136 | tf_op jit(solution)/shard_map/ppermute | solution.py:247
  347.9 15.8 %collective-permute-start.25 = (bf16[64,1792]{1,0:T(8,128)(2,1)S(1)}, bf16[64,1792]{1,0:T(8,128)(2,1)S(1)}, u32[]{:S(2)}, u32[]{:S(2)}) collective-permute-start(bf16[64,1792]{1,0:T(8,128)(2,1)S(1)} %shard_map.83), channel_id=1, source_target_pairs={{0,62},{1,63},{2,0},{3,1},{4,2},{5,3},{6,4},{7,5},{8,6},{9,7},{10,... | collective-permute-start | bytes 688136 | tf_op jit(solution)/shard_map/ppermute | solution.py:247
  349.4 14.4 %collective-permute-start.40 = (bf16[64,1792]{1,0:T(8,128)(2,1)S(1)}, bf16[64,1792]{1,0:T(8,128)(2,1)S(1)}, u32[]{:S(2)}, u32[]{:S(2)}) collective-permute-start(bf16[64,1792]{1,0:T(8,128)(2,1)S(1)} %shard_map.100), channel_id=1, source_target_pairs={{0,2},{1,3},{2,4},{3,5},{4,6},{5,7},{6,8},{7,9},{8,10},{9,11},{10,... | collective-permute-start | bytes 688136 | tf_op jit(solution)/shard_map/ppermute | solution.py:247
  351.9 14.1 %collective-permute-start.10 = (bf16[64,1792]{1,0:T(8,128)(2,1)S(1)}, bf16[64,1792]{1,0:T(8,128)(2,1)S(1)}, u32[]{:S(2)}, u32[]{:S(2)}) collective-permute-start(bf16[64,1792]{1,0:T(8,128)(2,1)S(1)} %shard_map.67), channel_id=1, source_target_pairs={{0,2},{1,3},{2,4},{3,5},{4,6},{5,7},{6,8},{7,9},{8,10},{9,11},{10,... | collective-permute-start | bytes 688136 | tf_op jit(solution)/shard_map/ppermute | solution.py:247
  360.3 14.3 %collective-permute-start.56 = (bf16[64,1792]{1,0:T(8,128)(2,1)S(1)}, bf16[64,1792]{1,0:T(8,128)(2,1)S(1)}, u32[]{:S(2)}, u32[]{:S(2)}) collective-permute-start(bf16[64,1792]{1,0:T(8,128)(2,1)S(1)} %shard_map.117), channel_id=1, source_target_pairs={{0,62},{1,63},{2,0},{3,1},{4,2},{5,3},{6,4},{7,5},{8,6},{9,7},{10,... | collective-permute-start | bytes 688136 | tf_op jit(solution)/shard_map/ppermute | solution.py:247
  363.7 14.4 %collective-permute-start.26 = (bf16[64,1792]{1,0:T(8,128)(2,1)S(1)}, bf16[64,1792]{1,0:T(8,128)(2,1)S(1)}, u32[]{:S(2)}, u32[]{:S(2)}) collective-permute-start(bf16[64,1792]{1,0:T(8,128)(2,1)S(1)} %shard_map.84), channel_id=1, source_target_pairs={{0,62},{1,63},{2,0},{3,1},{4,2},{5,3},{6,4},{7,5},{8,6},{9,7},{10,... | collective-permute-start | bytes 688136 | tf_op jit(solution)/shard_map/ppermute | solution.py:247
  363.9 14.4 %collective-permute-start.41 = (bf16[64,1792]{1,0:T(8,128)(2,1)S(1)}, bf16[64,1792]{1,0:T(8,128)(2,1)S(1)}, u32[]{:S(2)}, u32[]{:S(2)}) collective-permute-start(bf16[64,1792]{1,0:T(8,128)(2,1)S(1)} %shard_map.101), channel_id=1, source_target_pairs={{0,2},{1,3},{2,4},{3,5},{4,6},{5,7},{6,8},{7,9},{8,10},{9,11},{10,... | collective-permute-start | bytes 688136 | tf_op jit(solution)/shard_map/ppermute | solution.py:247
  366.1 14.4 %collective-permute-start.11 = (bf16[64,1792]{1,0:T(8,128)(2,1)S(1)}, bf16[64,1792]{1,0:T(8,128)(2,1)S(1)}, u32[]{:S(2)}, u32[]{:S(2)}) collective-permute-start(bf16[64,1792]{1,0:T(8,128)(2,1)S(1)} %shard_map.70), channel_id=1, source_target_pairs={{0,2},{1,3},{2,4},{3,5},{4,6},{5,7},{6,8},{7,9},{8,10},{9,11},{10,... | collective-permute-start | bytes 688136 | tf_op jit(solution)/shard_map/ppermute | solution.py:247
  378.2 10.8 %collective-permute-start.27 = (bf16[64,1792]{1,0:T(8,128)(2,1)S(1)}, bf16[64,1792]{1,0:T(8,128)(2,1)S(1)}, u32[]{:S(2)}, u32[]{:S(2)}) collective-permute-start(bf16[64,1792]{1,0:T(8,128)(2,1)S(1)} %shard_map.85), channel_id=1, source_target_pairs={{0,62},{1,63},{2,0},{3,1},{4,2},{5,3},{6,4},{7,5},{8,6},{9,7},{10,... | collective-permute-start | bytes 688136 | tf_op jit(solution)/shard_map/ppermute | solution.py:247
  378.4 14.5 %collective-permute-start.42 = (bf16[64,1792]{1,0:T(8,128)(2,1)S(1)}, bf16[64,1792]{1,0:T(8,128)(2,1)S(1)}, u32[]{:S(2)}, u32[]{:S(2)}) collective-permute-start(bf16[64,1792]{1,0:T(8,128)(2,1)S(1)} %shard_map.104), channel_id=1, source_target_pairs={{0,2},{1,3},{2,4},{3,5},{4,6},{5,7},{6,8},{7,9},{8,10},{9,11},{10,... | collective-permute-start | bytes 688136 | tf_op jit(solution)/shard_map/ppermute | solution.py:247
  380.6 12.5 %collective-permute-start.12 = (bf16[64,1792]{1,0:T(8,128)(2,1)S(1)}, bf16[64,1792]{1,0:T(8,128)(2,1)S(1)}, u32[]{:S(2)}, u32[]{:S(2)}) collective-permute-start(bf16[64,1792]{1,0:T(8,128)(2,1)S(1)} %shard_map.71), channel_id=1, source_target_pairs={{0,2},{1,3},{2,4},{3,5},{4,6},{5,7},{6,8},{7,9},{8,10},{9,11},{10,... | collective-permute-start | bytes 688136 | tf_op jit(solution)/shard_map/ppermute | solution.py:247
  384.1 9.8 %collective-permute-start.58 = (bf16[64,1792]{1,0:T(8,128)(2,1)S(1)}, bf16[64,1792]{1,0:T(8,128)(2,1)S(1)}, u32[]{:S(2)}, u32[]{:S(2)}) collective-permute-start(bf16[64,1792]{1,0:T(8,128)(2,1)S(1)} %shard_map.119), channel_id=1, source_target_pairs={{0,62},{1,63},{2,0},{3,1},{4,2},{5,3},{6,4},{7,5},{8,6},{9,7},{10,... | collective-permute-start | bytes 688136 | tf_op jit(solution)/shard_map/ppermute | solution.py:247
  389.1 9.8 %collective-permute-start.28 = (bf16[64,1792]{1,0:T(8,128)(2,1)S(1)}, bf16[64,1792]{1,0:T(8,128)(2,1)S(1)}, u32[]{:S(2)}, u32[]{:S(2)}) collective-permute-start(bf16[64,1792]{1,0:T(8,128)(2,1)S(1)} %shard_map.86), channel_id=1, source_target_pairs={{0,62},{1,63},{2,0},{3,1},{4,2},{5,3},{6,4},{7,5},{8,6},{9,7},{10,... | collective-permute-start | bytes 688136 | tf_op jit(solution)/shard_map/ppermute | solution.py:247
  392.9 9.8 %collective-permute-start.43 = (bf16[64,1792]{1,0:T(8,128)(2,1)S(1)}, bf16[64,1792]{1,0:T(8,128)(2,1)S(1)}, u32[]{:S(2)}, u32[]{:S(2)}) collective-permute-start(bf16[64,1792]{1,0:T(8,128)(2,1)S(1)} %shard_map.105), channel_id=1, source_target_pairs={{0,2},{1,3},{2,4},{3,5},{4,6},{5,7},{6,8},{7,9},{8,10},{9,11},{10,... | collective-permute-start | bytes 688136 | tf_op jit(solution)/shard_map/ppermute | solution.py:247
  393.2 11.8 %collective-permute-start.13 = (bf16[64,1792]{1,0:T(8,128)(2,1)S(1)}, bf16[64,1792]{1,0:T(8,128)(2,1)S(1)}, u32[]{:S(2)}, u32[]{:S(2)}) collective-permute-start(bf16[64,1792]{1,0:T(8,128)(2,1)S(1)} %shard_map.72), channel_id=1, source_target_pairs={{0,2},{1,3},{2,4},{3,5},{4,6},{5,7},{6,8},{7,9},{8,10},{9,11},{10,... | collective-permute-start | bytes 688136 | tf_op jit(solution)/shard_map/ppermute | solution.py:247
  394.0 12.9 %collective-permute-start.59 = (bf16[64,1792]{1,0:T(8,128)(2,1)S(1)}, bf16[64,1792]{1,0:T(8,128)(2,1)S(1)}, u32[]{:S(2)}, u32[]{:S(2)}) collective-permute-start(bf16[64,1792]{1,0:T(8,128)(2,1)S(1)} %shard_map.120), channel_id=1, source_target_pairs={{0,62},{1,63},{2,0},{3,1},{4,2},{5,3},{6,4},{7,5},{8,6},{9,7},{10,... | collective-permute-start | bytes 688136 | tf_op jit(solution)/shard_map/ppermute | solution.py:247
  398.9 9.9 %collective-permute-start.29 = (bf16[64,1792]{1,0:T(8,128)(2,1)S(1)}, bf16[64,1792]{1,0:T(8,128)(2,1)S(1)}, u32[]{:S(2)}, u32[]{:S(2)}) collective-permute-start(bf16[64,1792]{1,0:T(8,128)(2,1)S(1)} %shard_map.87), channel_id=1, source_target_pairs={{0,62},{1,63},{2,0},{3,1},{4,2},{5,3},{6,4},{7,5},{8,6},{9,7},{10,... | collective-permute-start | bytes 688136 | tf_op jit(solution)/shard_map/ppermute | solution.py:247
  402.8 9.8 %collective-permute-start.44 = (bf16[64,1792]{1,0:T(8,128)(2,1)S(1)}, bf16[64,1792]{1,0:T(8,128)(2,1)S(1)}, u32[]{:S(2)}, u32[]{:S(2)}) collective-permute-start(bf16[64,1792]{1,0:T(8,128)(2,1)S(1)} %shard_map.106), channel_id=1, source_target_pairs={{0,2},{1,3},{2,4},{3,5},{4,6},{5,7},{6,8},{7,9},{8,10},{9,11},{10,... | collective-permute-start | bytes 688136 | tf_op jit(solution)/shard_map/ppermute | solution.py:247
  405.1 12.2 %collective-permute-start.14 = (bf16[64,1792]{1,0:T(8,128)(2,1)S(1)}, bf16[64,1792]{1,0:T(8,128)(2,1)S(1)}, u32[]{:S(2)}, u32[]{:S(2)}) collective-permute-start(bf16[64,1792]{1,0:T(8,128)(2,1)S(1)} %shard_map.73), channel_id=1, source_target_pairs={{0,2},{1,3},{2,4},{3,5},{4,6},{5,7},{6,8},{7,9},{8,10},{9,11},{10,... | collective-permute-start | bytes 688136 | tf_op jit(solution)/shard_map/ppermute | solution.py:247
  407.0 10.5 %collective-permute-start.60 = (bf16[64,1792]{1,0:T(8,128)(2,1)S(1)}, bf16[64,1792]{1,0:T(8,128)(2,1)S(1)}, u32[]{:S(2)}, u32[]{:S(2)}) collective-permute-start(bf16[64,1792]{1,0:T(8,128)(2,1)S(1)} %shard_map.121), channel_id=1, source_target_pairs={{0,62},{1,63},{2,0},{3,1},{4,2},{5,3},{6,4},{7,5},{8,6},{9,7},{10,... | collective-permute-start | bytes 688136 | tf_op jit(solution)/shard_map/ppermute | solution.py:247
  408.9 12.0 %collective-permute-start.30 = (bf16[64,1792]{1,0:T(8,128)(2,1)S(1)}, bf16[64,1792]{1,0:T(8,128)(2,1)S(1)}, u32[]{:S(2)}, u32[]{:S(2)}) collective-permute-start(bf16[64,1792]{1,0:T(8,128)(2,1)S(1)} %shard_map.88), channel_id=1, source_target_pairs={{0,62},{1,63},{2,0},{3,1},{4,2},{5,3},{6,4},{7,5},{8,6},{9,7},{10,... | collective-permute-start | bytes 688136 | tf_op jit(solution)/shard_map/ppermute | solution.py:247
  (16 other events, 131.6 us)
where the time goes:
time: 446 us; the launch traced here: 437 us
  waiting for transfers between devices  250 us (56%)
  starting transfers between devices  130 us (29%)
  Pallas kernels  51.3 us (12%)
    all_to_all x1, waiting for transfers between devices, on_device(): lax.all_to_all(packed, 'ep', split_axis=0, concat_axis=0, axis_index_grou...  190 us
    ppermute x62, starting transfers between devices, shifted(): lax.ppermute(value, 'ep', [(i, (i + 2 * distance) % experts) for i in ran...  97.2 us
    ppermute x62, waiting for transfers between devices, shifted(): lax.ppermute(value, 'ep', [(i, (i + 2 * distance) % experts) for i in ran...  48.4 us
    pallas_call x10, Pallas kernels, expert_call(): pl.pallas_call(lambda *refs: expert_kernel(*refs, count=count, capacity=c...  42.6 us
    all_to_all x1, starting transfers between devices, on_device(): lax.all_to_all(packed, 'ep', split_axis=0, concat_axis=0, axis_index_grou...  32.7 us
    ppermute x1, waiting for transfers between devices, on_device(): lax.ppermute(weight, 'ep', [(i, i ^ 1) for i in range(experts)])  11.9 us
  transfers between devices with their start and end apart: 64, of which 23 were waited for; matrix products, arithmetic and copies ran while one was open for 0% of the time, Pallas kernels for 10%

commit v1 on v0

--- a/solution.py
+++ b/solution.py
@@ -6,8 +6,8 @@
 from jax.sharding import PartitionSpec as P
 
 CHAINS = 2
-STEPS = (4, 6, 6)
-PIECES = (1, 2, 2)
+STEPS = (4, 4, 4, 4)
+PIECES = (1, 2, 2, 2)
 PARTS = 4
 INTERPRET = False
 
@@ -157,11 +157,11 @@
     other = project(1 - core, other_weight)
     lower = jnp.where(core == 0, own, other)
     upper = jnp.where(core == 0, other, own)
-    lanes = 6 * capacity
+    lanes = 4 * capacity
     wanted = lax.broadcasted_iota(jnp.int32, (tokens, lanes), 0).astype(jnp.float32)
     for i, p in enumerate(packed):
         at = slice(i * capacity, (i + 1) * capacity)
-        stacked = jnp.concatenate([lower[at], upper[at]] * 3, axis=0)
+        stacked = jnp.concatenate([lower[at], upper[at]] * 2, axis=0)
         table = p[0, tiles * 2 * capacity :, :].astype(jnp.float32)
         scale = jnp.where(table[0:1, :lanes] == wanted, table[1:2, :lanes], 0.0).astype(jnp.bfloat16)
         out_ref[i] = jnp.dot(scale, stacked, preferred_element_type=jnp.float32).astype(

time: 446 us -> 453 us (1.016)
  Pallas kernels: 51.3 us -> 62.7 us
    pallas_call x10 -> x14, Pallas kernels: 42.6 us -> 54 us  [expert_call(): pl.pallas_call(lambda *refs: expert_kernel(*refs, count=count, capacity=c...]
  transfers between devices with their start and end apart: 64 -> 64, of which waited for: 23 -> 25; matrix products, arithmetic and copies ran while one was open for 0% -> 0% of each run, Pallas kernels for 10% -> 12%
where the time goes in v1:
time: 453 us; the launch traced here: 444 us
  waiting for transfers between devices  246 us (54%)
  starting transfers between devices  130 us (29%)
  Pallas kernels  62.7 us (14%)
    all_to_all x1, waiting for transfers between devices, on_device(): lax.all_to_all(packed, 'ep', split_axis=0, concat_axis=0, axis_index_grou...  190 us
    ppermute x62, starting transfers between devices, shifted(): lax.ppermute(value, 'ep', [(i, (i + 2 * distance) % experts) for i in ran...  97 us
    pallas_call x14, Pallas kernels, expert_call(): pl.pallas_call(lambda *refs: expert_kernel(*refs, count=count, capacity=c...  54 us
    ppermute x62, waiting for transfers between devices, shifted(): lax.ppermute(value, 'ep', [(i, (i + 2 * distance) % experts) for i in ran...  44 us
    all_to_all x1, starting transfers between devices, on_device(): lax.all_to_all(packed, 'ep', split_axis=0, concat_axis=0, axis_index_grou...  32.7 us
    ppermute x1, waiting for transfers between devices, on_device(): lax.ppermute(weight, 'ep', [(i, i ^ 1) for i in range(experts)])  11.9 us
  transfers between devices with their start and end apart: 64, of which 25 were waited for; matrix products, arithmetic and copies ran while one was open for 0% of the time, Pallas kernels for 12%

profile of v1, /device:TPU:46, one launch (start us, length us, event | category | flops | bytes accessed | tf_op | source)
XLA Modules:
  0.0 444.1 jit_solution(12791393177562596989)
XLA Ops:
  3.6 4.5 %shard_map.55 = bf16[32,264,128]{2,1,0:T(8,128)(2,1)} custom-call(s32[1,512]{1,0:T(1,128)} %reshape.9.refs_0_, f32[1,512]{1,0:T(1,128)} %reshape.10.refs_1_, bf16[512,2048]{1,0:T(8,128)(2,1)} %bitcast.37), custom_call_target="tpu_custom_call" | custom-call | tf_op jit(solution)/shard_map/pallas_call | solution.py:113
  8.0 32.7 %all-to-all-start = ((bf16[32,264,128]{2,1,0:T(8,128)(2,1)}), bf16[32,264,128]{2,1,0:T(8,128)(2,1)S(1)}, u32[]{:S(2)}, u32[]{:S(2)}) async-start(bf16[32,264,128]{2,1,0:T(8,128)(2,1)} %shard_map.55), calls=%async_computation | async-start | bytes 4325376 | tf_op jit(solution)/shard_map/all_to_all | solution.py:262
  41.0 11.9 %collective-permute-done.refs_10_ = bf16[1024,3584]{1,0:T(8,128)(2,1)} collective-permute-done((bf16[1024,3584]{1,0:T(8,128)(2,1)}, bf16[1024,3584]{1,0:T(8,128)(2,1)}, u32[]{:S(2)}, u32[]{:S(2)}) %collective-permute-start) | collective-permute-done | bytes 7340064 | tf_op jit(solution)/shard_map/ppermute | solution.py:261
  52.8 189.7 %all-to-all-done.refs_1_.refs_2_.refs_3_.refs_4_.refs_5_.refs_6_.refs_7_.refs_8_ = bf16[32,264,128]{2,1,0:T(8,128)(2,1)S(1)} async-done(((bf16[32,264,128]{2,1,0:T(8,128)(2,1)}), bf16[32,264,128]{2,1,0:T(8,128)(2,1)S(1)}, u32[]{:S(2)}, u32[]{:S(2)}) %all-to-all-start) | async-done | bytes 2162720 | tf_op jit(solution)/shard_map/all_to_all | solution.py:262
  242.6 4.9 %shard_map.56.refs_0_ = bf16[8,64,1792]{2,1,0:T(8,128)(2,1)S(1)} custom-call(s32[2]{0:T(128)S(1)} %pad_add_fusion.refs_0_, bf16[32,264,128]{2,1,0:T(8,128)(2,1)S(1)} %all-to-all-done.refs_1_.refs_2_.refs_3_.refs_4_.refs_5_.refs_6_.refs_7_.refs_8_, bf16[32,264,128]{2,1,0:T(8,128)(2,1)S(1)} %all-to-all-done.refs_1_.refs_2_.refs_3_.refs_4_.refs_5_.refs_6_.refs_7_.refs_8_, ...), custom_call_target="tpu_custom_call" | custom-call | flops 939524096 | bytes 7340032 | tf_op jit(solution)/shard_map/pallas_call | solution.py:193
  247.7 3.2 collective-permute-start.17
  250.9 4.9 %shard_map.92.refs_0_ = bf16[8,64,1792]{2,1,0:T(8,128)(2,1)S(1)} custom-call(s32[2]{0:T(128)S(1)} %pad_add_fusion.refs_0_, bf16[32,264,128]{2,1,0:T(8,128)(2,1)S(1)} %all-to-all-done.refs_1_.refs_2_.refs_3_.refs_4_.refs_5_.refs_6_.refs_7_.refs_8_, bf16[32,264,128]{2,1,0:T(8,128)(2,1)S(1)} %all-to-all-done.refs_1_.refs_2_.refs_3_.refs_4_.refs_5_.refs_6_.refs_7_.refs_8_, ...), custom_call_target="tpu_custom_call" | custom-call | flops 939524096 | bytes 7340032 | tf_op jit(solution)/shard_map/pallas_call | solution.py:193
  256.2 3.3 collective-permute-start.48
  261.6 3.4 collective-permute-done.32.left_ref
  265.5 4.5 %collective-permute-done.2.left_ref = bf16[64,1792]{1,0:T(8,128)(2,1)S(1)} collective-permute-done((bf16[64,1792]{1,0:T(8,128)(2,1)S(1)}, bf16[64,1792]{1,0:T(8,128)(2,1)S(1)}, u32[]{:S(2)}, u32[]{:S(2)}) %collective-permute-start.2) | collective-permute-done | bytes 229408 | tf_op jit(solution)/shard_map/ppermute | solution.py:247
  270.3 3.3 collective-permute-start.49
  276.0 4.1 collective-permute-done.3.left_ref
  280.3 3.7 shard_map.60.refs_0_
  283.9 3.7 shard_map.61.refs_1_
  287.7 3.3 collective-permute-start.50
  293.7 3.7 shard_map.96.refs_0_
  297.4 3.7 shard_map.97.refs_1_
  301.2 3.7 collective-permute-start.51
  307.5 3.3 collective-permute-done.51.left_ref
  310.9 3.8 collective-permute-start.52
  315.9 3.8 collective-permute-start.22
  320.8 3.8 collective-permute-start.53
  330.2 3.7 shard_map.66.refs_0_
  333.9 3.7 shard_map.67.refs_1_
  337.7 3.3 collective-permute-start.54
  343.8 3.7 shard_map.102.refs_0_
  347.5 3.7 shard_map.103.refs_1_
  351.3 3.3 collective-permute-start.55
  357.3 3.3 collective-permute-done.55.left_ref
  360.6 3.8 collective-permute-start.56
  365.5 3.8 collective-permute-start.26
  370.5 3.8 collective-permute-start.57
  374.4 2.6 collective-permute-start.27
  379.5 3.7 shard_map.72.refs_0_
  383.2 3.7 shard_map.73.refs_1_
  386.9 3.3 collective-permute-start.58
  392.9 3.7 shard_map.108.refs_0_
  396.6 3.7 shard_map.109.refs_1_
  400.4 3.3 collective-permute-start.59
  406.6 3.1 collective-permute-done.59.left_ref
  409.7 3.8 collective-permute-start.60
  414.7 3.8 collective-permute-start.30
  419.5 3.8 collective-permute-start.61
  424.1 3.8 collective-permute-start.31
  428.2 2.7 collective-permute-done.15.left_ref
  431.2 3.3 collective-permute-start.62
  435.6 2.6 collective-permute-done.16
  438.3 4.5 %collective-permute-done.47 = bf16[64,1792]{1,0:T(8,128)(2,1)S(1)} collective-permute-done((bf16[64,1792]{1,0:T(8,128)(2,1)S(1)}, bf16[64,1792]{1,0:T(8,128)(2,1)S(1)}, u32[]{:S(2)}, u32[]{:S(2)}) %collective-permute-start.47) | collective-permute-done | bytes 229408 | tf_op jit(solution)/shard_map/ppermute | solution.py:247
  (166 shorter events, 43.9 us)
Async XLA Ops:
  8.0 234.5 %all-to-all-start = ((bf16[32,264,128]{2,1,0:T(8,128)(2,1)}), bf16[32,264,128]{2,1,0:T(8,128)(2,1)S(1)}, u32[]{:S(2)}, u32[]{:S(2)}) async-start(bf16[32,264,128]{2,1,0:T(8,128)(2,1)} %shard_map.55), calls=%async_computation | async-start | bytes 4325376 | tf_op jit(solution)/shard_map/all_to_all | solution.py:262
  40.7 12.1 %collective-permute-start = (bf16[1024,3584]{1,0:T(8,128)(2,1)}, bf16[1024,3584]{1,0:T(8,128)(2,1)}, u32[]{:S(2)}, u32[]{:S(2)}) collective-permute-start(bf16[1024,3584]{1,0:T(8,128)(2,1)} %bitcast.22), channel_id=1, source_target_pairs={{0,1},{1,0},{2,3},{3,2},{4,5},{5,4},{6,7},{7,6},{8,9},{9,8},{10,11... | collective-permute-start | bytes 22020104 | tf_op jit(solution)/shard_map/ppermute | solution.py:261
  247.7 11.9 %collective-permute-start.17 = (bf16[64,1792]{1,0:T(8,128)(2,1)S(1)}, bf16[64,1792]{1,0:T(8,128)(2,1)S(1)}, u32[]{:S(2)}, u32[]{:S(2)}) collective-permute-start(bf16[64,1792]{1,0:T(8,128)(2,1)S(1)} %get-tuple-element.6), channel_id=1, source_target_pairs={{0,62},{1,63},{2,0},{3,1},{4,2},{5,3},{6,4},{7,5},{8,6},{9,7},{10,... | collective-permute-start | bytes 688136 | tf_op jit(solution)/shard_map/ppermute | solution.py:247
  256.1 13.9 %collective-permute-start.2 = (bf16[64,1792]{1,0:T(8,128)(2,1)S(1)}, bf16[64,1792]{1,0:T(8,128)(2,1)S(1)}, u32[]{:S(2)}, u32[]{:S(2)}) collective-permute-start(bf16[64,1792]{1,0:T(8,128)(2,1)S(1)} %shard_map.57), channel_id=1, source_target_pairs={{0,2},{1,3},{2,4},{3,5},{4,6},{5,7},{6,8},{7,9},{8,10},{9,11},{10,... | collective-permute-start | bytes 688136 | tf_op jit(solution)/shard_map/ppermute | solution.py:247
  256.2 13.9 %collective-permute-start.48 = (bf16[64,1792]{1,0:T(8,128)(2,1)S(1)}, bf16[64,1792]{1,0:T(8,128)(2,1)S(1)}, u32[]{:S(2)}, u32[]{:S(2)}) collective-permute-start(bf16[64,1792]{1,0:T(8,128)(2,1)S(1)} %get-tuple-element.8), channel_id=1, source_target_pairs={{0,62},{1,63},{2,0},{3,1},{4,2},{5,3},{6,4},{7,5},{8,6},{9,7},{10,... | collective-permute-start | bytes 688136 | tf_op jit(solution)/shard_map/ppermute | solution.py:247
  259.6 14.0 %collective-permute-start.18 = (bf16[64,1792]{1,0:T(8,128)(2,1)S(1)}, bf16[64,1792]{1,0:T(8,128)(2,1)S(1)}, u32[]{:S(2)}, u32[]{:S(2)}) collective-permute-start(bf16[64,1792]{1,0:T(8,128)(2,1)S(1)} %shard_map.78), channel_id=1, source_target_pairs={{0,62},{1,63},{2,0},{3,1},{4,2},{5,3},{6,4},{7,5},{8,6},{9,7},{10,... | collective-permute-start | bytes 688136 | tf_op jit(solution)/shard_map/ppermute | solution.py:247
  265.1 10.0 %collective-permute-start.33 = (bf16[64,1792]{1,0:T(8,128)(2,1)S(1)}, bf16[64,1792]{1,0:T(8,128)(2,1)S(1)}, u32[]{:S(2)}, u32[]{:S(2)}) collective-permute-start(bf16[64,1792]{1,0:T(8,128)(2,1)S(1)} %shard_map.93), channel_id=1, source_target_pairs={{0,2},{1,3},{2,4},{3,5},{4,6},{5,7},{6,8},{7,9},{8,10},{9,11},{10,... | collective-permute-start | bytes 688136 | tf_op jit(solution)/shard_map/ppermute | solution.py:247
  270.0 10.0 %collective-permute-start.3 = (bf16[64,1792]{1,0:T(8,128)(2,1)S(1)}, bf16[64,1792]{1,0:T(8,128)(2,1)S(1)}, u32[]{:S(2)}, u32[]{:S(2)}) collective-permute-start(bf16[64,1792]{1,0:T(8,128)(2,1)S(1)} %shard_map.58), channel_id=1, source_target_pairs={{0,2},{1,3},{2,4},{3,5},{4,6},{5,7},{6,8},{7,9},{8,10},{9,11},{10,... | collective-permute-start | bytes 688136 | tf_op jit(solution)/shard_map/ppermute | solution.py:247
  270.3 17.4 %collective-permute-start.49 = (bf16[64,1792]{1,0:T(8,128)(2,1)S(1)}, bf16[64,1792]{1,0:T(8,128)(2,1)S(1)}, u32[]{:S(2)}, u32[]{:S(2)}) collective-permute-start(bf16[64,1792]{1,0:T(8,128)(2,1)S(1)} %shard_map.114), channel_id=1, source_target_pairs={{0,62},{1,63},{2,0},{3,1},{4,2},{5,3},{6,4},{7,5},{8,6},{9,7},{10,... | collective-permute-start | bytes 688136 | tf_op jit(solution)/shard_map/ppermute | solution.py:247
  273.6 17.4 %collective-permute-start.19 = (bf16[64,1792]{1,0:T(8,128)(2,1)S(1)}, bf16[64,1792]{1,0:T(8,128)(2,1)S(1)}, u32[]{:S(2)}, u32[]{:S(2)}) collective-permute-start(bf16[64,1792]{1,0:T(8,128)(2,1)S(1)} %shard_map.79), channel_id=1, source_target_pairs={{0,62},{1,63},{2,0},{3,1},{4,2},{5,3},{6,4},{7,5},{8,6},{9,7},{10,... | collective-permute-start | bytes 688136 | tf_op jit(solution)/shard_map/ppermute | solution.py:247
  275.2 16.1 %collective-permute-start.34 = (bf16[64,1792]{1,0:T(8,128)(2,1)S(1)}, bf16[64,1792]{1,0:T(8,128)(2,1)S(1)}, u32[]{:S(2)}, u32[]{:S(2)}) collective-permute-start(bf16[64,1792]{1,0:T(8,128)(2,1)S(1)} %shard_map.94), channel_id=1, source_target_pairs={{0,2},{1,3},{2,4},{3,5},{4,6},{5,7},{6,8},{7,9},{8,10},{9,11},{10,... | collective-permute-start | bytes 688136 | tf_op jit(solution)/shard_map/ppermute | solution.py:247
  280.1 13.3 %collective-permute-start.4 = (bf16[64,1792]{1,0:T(8,128)(2,1)S(1)}, bf16[64,1792]{1,0:T(8,128)(2,1)S(1)}, u32[]{:S(2)}, u32[]{:S(2)}) collective-permute-start(bf16[64,1792]{1,0:T(8,128)(2,1)S(1)} %shard_map.59), channel_id=1, source_target_pairs={{0,2},{1,3},{2,4},{3,5},{4,6},{5,7},{6,8},{7,9},{8,10},{9,11},{10,... | collective-permute-start | bytes 688136 | tf_op jit(solution)/shard_map/ppermute | solution.py:247
  287.7 13.3 %collective-permute-start.50 = (bf16[64,1792]{1,0:T(8,128)(2,1)S(1)}, bf16[64,1792]{1,0:T(8,128)(2,1)S(1)}, u32[]{:S(2)}, u32[]{:S(2)}) collective-permute-start(bf16[64,1792]{1,0:T(8,128)(2,1)S(1)} %shard_map.115), channel_id=1, source_target_pairs={{0,62},{1,63},{2,0},{3,1},{4,2},{5,3},{6,4},{7,5},{8,6},{9,7},{10,... | collective-permute-start | bytes 688136 | tf_op jit(solution)/shard_map/ppermute | solution.py:247
  291.1 13.7 %collective-permute-start.20 = (bf16[64,1792]{1,0:T(8,128)(2,1)S(1)}, bf16[64,1792]{1,0:T(8,128)(2,1)S(1)}, u32[]{:S(2)}, u32[]{:S(2)}) collective-permute-start(bf16[64,1792]{1,0:T(8,128)(2,1)S(1)} %shard_map.80), channel_id=1, source_target_pairs={{0,62},{1,63},{2,0},{3,1},{4,2},{5,3},{6,4},{7,5},{8,6},{9,7},{10,... | collective-permute-start | bytes 688136 | tf_op jit(solution)/shard_map/ppermute | solution.py:247
  291.4 13.8 %collective-permute-start.35 = (bf16[64,1792]{1,0:T(8,128)(2,1)S(1)}, bf16[64,1792]{1,0:T(8,128)(2,1)S(1)}, u32[]{:S(2)}, u32[]{:S(2)}) collective-permute-start(bf16[64,1792]{1,0:T(8,128)(2,1)S(1)} %shard_map.95), channel_id=1, source_target_pairs={{0,2},{1,3},{2,4},{3,5},{4,6},{5,7},{6,8},{7,9},{8,10},{9,11},{10,... | collective-permute-start | bytes 688136 | tf_op jit(solution)/shard_map/ppermute | solution.py:247
  293.5 13.8 %collective-permute-start.5 = (bf16[64,1792]{1,0:T(8,128)(2,1)S(1)}, bf16[64,1792]{1,0:T(8,128)(2,1)S(1)}, u32[]{:S(2)}, u32[]{:S(2)}) collective-permute-start(bf16[64,1792]{1,0:T(8,128)(2,1)S(1)} %shard_map.62), channel_id=1, source_target_pairs={{0,2},{1,3},{2,4},{3,5},{4,6},{5,7},{6,8},{7,9},{8,10},{9,11},{10,... | collective-permute-start | bytes 688136 | tf_op jit(solution)/shard_map/ppermute | solution.py:247
  301.2 9.7 %collective-permute-start.51 = (bf16[64,1792]{1,0:T(8,128)(2,1)S(1)}, bf16[64,1792]{1,0:T(8,128)(2,1)S(1)}, u32[]{:S(2)}, u32[]{:S(2)}) collective-permute-start(bf16[64,1792]{1,0:T(8,128)(2,1)S(1)} %shard_map.116), channel_id=1, source_target_pairs={{0,62},{1,63},{2,0},{3,1},{4,2},{5,3},{6,4},{7,5},{8,6},{9,7},{10,... | collective-permute-start | bytes 688136 | tf_op jit(solution)/shard_map/ppermute | solution.py:247
  304.9 10.8 %collective-permute-start.21 = (bf16[64,1792]{1,0:T(8,128)(2,1)S(1)}, bf16[64,1792]{1,0:T(8,128)(2,1)S(1)}, u32[]{:S(2)}, u32[]{:S(2)}) collective-permute-start(bf16[64,1792]{1,0:T(8,128)(2,1)S(1)} %shard_map.81), channel_id=1, source_target_pairs={{0,62},{1,63},{2,0},{3,1},{4,2},{5,3},{6,4},{7,5},{8,6},{9,7},{10,... | collective-permute-start | bytes 688136 | tf_op jit(solution)/shard_map/ppermute | solution.py:247
  305.2 14.5 %collective-permute-start.36 = (bf16[64,1792]{1,0:T(8,128)(2,1)S(1)}, bf16[64,1792]{1,0:T(8,128)(2,1)S(1)}, u32[]{:S(2)}, u32[]{:S(2)}) collective-permute-start(bf16[64,1792]{1,0:T(8,128)(2,1)S(1)} %shard_map.98), channel_id=1, source_target_pairs={{0,2},{1,3},{2,4},{3,5},{4,6},{5,7},{6,8},{7,9},{8,10},{9,11},{10,... | collective-permute-start | bytes 688136 | tf_op jit(solution)/shard_map/ppermute | solution.py:247
  307.4 12.5 %collective-permute-start.6 = (bf16[64,1792]{1,0:T(8,128)(2,1)S(1)}, bf16[64,1792]{1,0:T(8,128)(2,1)S(1)}, u32[]{:S(2)}, u32[]{:S(2)}) collective-permute-start(bf16[64,1792]{1,0:T(8,128)(2,1)S(1)} %shard_map.63), channel_id=1, source_target_pairs={{0,2},{1,3},{2,4},{3,5},{4,6},{5,7},{6,8},{7,9},{8,10},{9,11},{10,... | collective-permute-start | bytes 688136 | tf_op jit(solution)/shard_map/ppermute | solution.py:247
  310.9 9.8 %collective-permute-start.52 = (bf16[64,1792]{1,0:T(8,128)(2,1)S(1)}, bf16[64,1792]{1,0:T(8,128)(2,1)S(1)}, u32[]{:S(2)}, u32[]{:S(2)}) collective-permute-start(bf16[64,1792]{1,0:T(8,128)(2,1)S(1)} %shard_map.117), channel_id=1, source_target_pairs={{0,62},{1,63},{2,0},{3,1},{4,2},{5,3},{6,4},{7,5},{8,6},{9,7},{10,... | collective-permute-start | bytes 688136 | tf_op jit(solution)/shard_map/ppermute | solution.py:247
  320.0 10.0 %collective-permute-start.7 = (bf16[64,1792]{1,0:T(8,128)(2,1)S(1)}, bf16[64,1792]{1,0:T(8,128)(2,1)S(1)}, u32[]{:S(2)}, u32[]{:S(2)}) collective-permute-start(bf16[64,1792]{1,0:T(8,128)(2,1)S(1)} %shard_map.64), channel_id=1, source_target_pairs={{0,2},{1,3},{2,4},{3,5},{4,6},{5,7},{6,8},{7,9},{8,10},{9,11},{10,... | collective-permute-start | bytes 688136 | tf_op jit(solution)/shard_map/ppermute | solution.py:247
  320.8 16.8 %collective-permute-start.53 = (bf16[64,1792]{1,0:T(8,128)(2,1)S(1)}, bf16[64,1792]{1,0:T(8,128)(2,1)S(1)}, u32[]{:S(2)}, u32[]{:S(2)}) collective-permute-start(bf16[64,1792]{1,0:T(8,128)(2,1)S(1)} %shard_map.118), channel_id=1, source_target_pairs={{0,62},{1,63},{2,0},{3,1},{4,2},{5,3},{6,4},{7,5},{8,6},{9,7},{10,... | collective-permute-start | bytes 688136 | tf_op jit(solution)/shard_map/ppermute | solution.py:247
  324.7 16.3 %collective-permute-start.23 = (bf16[64,1792]{1,0:T(8,128)(2,1)S(1)}, bf16[64,1792]{1,0:T(8,128)(2,1)S(1)}, u32[]{:S(2)}, u32[]{:S(2)}) collective-permute-start(bf16[64,1792]{1,0:T(8,128)(2,1)S(1)} %shard_map.83), channel_id=1, source_target_pairs={{0,62},{1,63},{2,0},{3,1},{4,2},{5,3},{6,4},{7,5},{8,6},{9,7},{10,... | collective-permute-start | bytes 688136 | tf_op jit(solution)/shard_map/ppermute | solution.py:247
  327.6 13.8 %collective-permute-start.38 = (bf16[64,1792]{1,0:T(8,128)(2,1)S(1)}, bf16[64,1792]{1,0:T(8,128)(2,1)S(1)}, u32[]{:S(2)}, u32[]{:S(2)}) collective-permute-start(bf16[64,1792]{1,0:T(8,128)(2,1)S(1)} %shard_map.100), channel_id=1, source_target_pairs={{0,2},{1,3},{2,4},{3,5},{4,6},{5,7},{6,8},{7,9},{8,10},{9,11},{10,... | collective-permute-start | bytes 688136 | tf_op jit(solution)/shard_map/ppermute | solution.py:247
  330.1 13.5 %collective-permute-start.8 = (bf16[64,1792]{1,0:T(8,128)(2,1)S(1)}, bf16[64,1792]{1,0:T(8,128)(2,1)S(1)}, u32[]{:S(2)}, u32[]{:S(2)}) collective-permute-start(bf16[64,1792]{1,0:T(8,128)(2,1)S(1)} %shard_map.65), channel_id=1, source_target_pairs={{0,2},{1,3},{2,4},{3,5},{4,6},{5,7},{6,8},{7,9},{8,10},{9,11},{10,... | collective-permute-start | bytes 688136 | tf_op jit(solution)/shard_map/ppermute | solution.py:247
  337.7 13.5 %collective-permute-start.54 = (bf16[64,1792]{1,0:T(8,128)(2,1)S(1)}, bf16[64,1792]{1,0:T(8,128)(2,1)S(1)}, u32[]{:S(2)}, u32[]{:S(2)}) collective-permute-start(bf16[64,1792]{1,0:T(8,128)(2,1)S(1)} %shard_map.119), channel_id=1, source_target_pairs={{0,62},{1,63},{2,0},{3,1},{4,2},{5,3},{6,4},{7,5},{8,6},{9,7},{10,... | collective-permute-start | bytes 688136 | tf_op jit(solution)/shard_map/ppermute | solution.py:247
  341.1 13.5 %collective-permute-start.24 = (bf16[64,1792]{1,0:T(8,128)(2,1)S(1)}, bf16[64,1792]{1,0:T(8,128)(2,1)S(1)}, u32[]{:S(2)}, u32[]{:S(2)}) collective-permute-start(bf16[64,1792]{1,0:T(8,128)(2,1)S(1)} %shard_map.84), channel_id=1, source_target_pairs={{0,62},{1,63},{2,0},{3,1},{4,2},{5,3},{6,4},{7,5},{8,6},{9,7},{10,... | collective-permute-start | bytes 688136 | tf_op jit(solution)/shard_map/ppermute | solution.py:247
  341.5 14.3 %collective-permute-start.39 = (bf16[64,1792]{1,0:T(8,128)(2,1)S(1)}, bf16[64,1792]{1,0:T(8,128)(2,1)S(1)}, u32[]{:S(2)}, u32[]{:S(2)}) collective-permute-start(bf16[64,1792]{1,0:T(8,128)(2,1)S(1)} %shard_map.101), channel_id=1, source_target_pairs={{0,2},{1,3},{2,4},{3,5},{4,6},{5,7},{6,8},{7,9},{8,10},{9,11},{10,... | collective-permute-start | bytes 688136 | tf_op jit(solution)/shard_map/ppermute | solution.py:247
  343.7 13.4 %collective-permute-start.9 = (bf16[64,1792]{1,0:T(8,128)(2,1)S(1)}, bf16[64,1792]{1,0:T(8,128)(2,1)S(1)}, u32[]{:S(2)}, u32[]{:S(2)}) collective-permute-start(bf16[64,1792]{1,0:T(8,128)(2,1)S(1)} %shard_map.68), channel_id=1, source_target_pairs={{0,2},{1,3},{2,4},{3,5},{4,6},{5,7},{6,8},{7,9},{8,10},{9,11},{10,... | collective-permute-start | bytes 688136 | tf_op jit(solution)/shard_map/ppermute | solution.py:247
  354.7 10.8 %collective-permute-start.25 = (bf16[64,1792]{1,0:T(8,128)(2,1)S(1)}, bf16[64,1792]{1,0:T(8,128)(2,1)S(1)}, u32[]{:S(2)}, u32[]{:S(2)}) collective-permute-start(bf16[64,1792]{1,0:T(8,128)(2,1)S(1)} %shard_map.85), channel_id=1, source_target_pairs={{0,62},{1,63},{2,0},{3,1},{4,2},{5,3},{6,4},{7,5},{8,6},{9,7},{10,... | collective-permute-start | bytes 688136 | tf_op jit(solution)/shard_map/ppermute | solution.py:247
  355.9 13.5 %collective-permute-start.40 = (bf16[64,1792]{1,0:T(8,128)(2,1)S(1)}, bf16[64,1792]{1,0:T(8,128)(2,1)S(1)}, u32[]{:S(2)}, u32[]{:S(2)}) collective-permute-start(bf16[64,1792]{1,0:T(8,128)(2,1)S(1)} %shard_map.104), channel_id=1, source_target_pairs={{0,2},{1,3},{2,4},{3,5},{4,6},{5,7},{6,8},{7,9},{8,10},{9,11},{10,... | collective-permute-start | bytes 688136 | tf_op jit(solution)/shard_map/ppermute | solution.py:247
  357.1 12.7 %collective-permute-start.10 = (bf16[64,1792]{1,0:T(8,128)(2,1)S(1)}, bf16[64,1792]{1,0:T(8,128)(2,1)S(1)}, u32[]{:S(2)}, u32[]{:S(2)}) collective-permute-start(bf16[64,1792]{1,0:T(8,128)(2,1)S(1)} %shard_map.69), channel_id=1, source_target_pairs={{0,2},{1,3},{2,4},{3,5},{4,6},{5,7},{6,8},{7,9},{8,10},{9,11},{10,... | collective-permute-start | bytes 688136 | tf_op jit(solution)/shard_map/ppermute | solution.py:247
  360.6 9.8 %collective-permute-start.56 = (bf16[64,1792]{1,0:T(8,128)(2,1)S(1)}, bf16[64,1792]{1,0:T(8,128)(2,1)S(1)}, u32[]{:S(2)}, u32[]{:S(2)}) collective-permute-start(bf16[64,1792]{1,0:T(8,128)(2,1)S(1)} %shard_map.121), channel_id=1, source_target_pairs={{0,62},{1,63},{2,0},{3,1},{4,2},{5,3},{6,4},{7,5},{8,6},{9,7},{10,... | collective-permute-start | bytes 688136 | tf_op jit(solution)/shard_map/ppermute | solution.py:247
  370.5 16.3 %collective-permute-start.57 = (bf16[64,1792]{1,0:T(8,128)(2,1)S(1)}, bf16[64,1792]{1,0:T(8,128)(2,1)S(1)}, u32[]{:S(2)}, u32[]{:S(2)}) collective-permute-start(bf16[64,1792]{1,0:T(8,128)(2,1)S(1)} %shard_map.122), channel_id=1, source_target_pairs={{0,62},{1,63},{2,0},{3,1},{4,2},{5,3},{6,4},{7,5},{8,6},{9,7},{10,... | collective-permute-start | bytes 688136 | tf_op jit(solution)/shard_map/ppermute | solution.py:247
  374.4 15.9 %collective-permute-start.27 = (bf16[64,1792]{1,0:T(8,128)(2,1)S(1)}, bf16[64,1792]{1,0:T(8,128)(2,1)S(1)}, u32[]{:S(2)}, u32[]{:S(2)}) collective-permute-start(bf16[64,1792]{1,0:T(8,128)(2,1)S(1)} %shard_map.87), channel_id=1, source_target_pairs={{0,62},{1,63},{2,0},{3,1},{4,2},{5,3},{6,4},{7,5},{8,6},{9,7},{10,... | collective-permute-start | bytes 688136 | tf_op jit(solution)/shard_map/ppermute | solution.py:247
  377.1 13.4 %collective-permute-start.42 = (bf16[64,1792]{1,0:T(8,128)(2,1)S(1)}, bf16[64,1792]{1,0:T(8,128)(2,1)S(1)}, u32[]{:S(2)}, u32[]{:S(2)}) collective-permute-start(bf16[64,1792]{1,0:T(8,128)(2,1)S(1)} %shard_map.106), channel_id=1, source_target_pairs={{0,2},{1,3},{2,4},{3,5},{4,6},{5,7},{6,8},{7,9},{8,10},{9,11},{10,... | collective-permute-start | bytes 688136 | tf_op jit(solution)/shard_map/ppermute | solution.py:247
  379.3 13.3 %collective-permute-start.12 = (bf16[64,1792]{1,0:T(8,128)(2,1)S(1)}, bf16[64,1792]{1,0:T(8,128)(2,1)S(1)}, u32[]{:S(2)}, u32[]{:S(2)}) collective-permute-start(bf16[64,1792]{1,0:T(8,128)(2,1)S(1)} %shard_map.71), channel_id=1, source_target_pairs={{0,2},{1,3},{2,4},{3,5},{4,6},{5,7},{6,8},{7,9},{8,10},{9,11},{10,... | collective-permute-start | bytes 688136 | tf_op jit(solution)/shard_map/ppermute | solution.py:247
  386.9 13.3 %collective-permute-start.58 = (bf16[64,1792]{1,0:T(8,128)(2,1)S(1)}, bf16[64,1792]{1,0:T(8,128)(2,1)S(1)}, u32[]{:S(2)}, u32[]{:S(2)}) collective-permute-start(bf16[64,1792]{1,0:T(8,128)(2,1)S(1)} %shard_map.123), channel_id=1, source_target_pairs={{0,62},{1,63},{2,0},{3,1},{4,2},{5,3},{6,4},{7,5},{8,6},{9,7},{10,... | collective-permute-start | bytes 688136 | tf_op jit(solution)/shard_map/ppermute | solution.py:247
  390.3 13.3 %collective-permute-start.28 = (bf16[64,1792]{1,0:T(8,128)(2,1)S(1)}, bf16[64,1792]{1,0:T(8,128)(2,1)S(1)}, u32[]{:S(2)}, u32[]{:S(2)}) collective-permute-start(bf16[64,1792]{1,0:T(8,128)(2,1)S(1)} %shard_map.88), channel_id=1, source_target_pairs={{0,62},{1,63},{2,0},{3,1},{4,2},{5,3},{6,4},{7,5},{8,6},{9,7},{10,... | collective-permute-start | bytes 688136 | tf_op jit(solution)/shard_map/ppermute | solution.py:247
  390.6 14.5 %collective-permute-start.43 = (bf16[64,1792]{1,0:T(8,128)(2,1)S(1)}, bf16[64,1792]{1,0:T(8,128)(2,1)S(1)}, u32[]{:S(2)}, u32[]{:S(2)}) collective-permute-start(bf16[64,1792]{1,0:T(8,128)(2,1)S(1)} %shard_map.107), channel_id=1, source_target_pairs={{0,2},{1,3},{2,4},{3,5},{4,6},{5,7},{6,8},{7,9},{8,10},{9,11},{10,... | collective-permute-start | bytes 688136 | tf_op jit(solution)/shard_map/ppermute | solution.py:247
  392.7 13.3 %collective-permute-start.13 = (bf16[64,1792]{1,0:T(8,128)(2,1)S(1)}, bf16[64,1792]{1,0:T(8,128)(2,1)S(1)}, u32[]{:S(2)}, u32[]{:S(2)}) collective-permute-start(bf16[64,1792]{1,0:T(8,128)(2,1)S(1)} %shard_map.74), channel_id=1, source_target_pairs={{0,2},{1,3},{2,4},{3,5},{4,6},{5,7},{6,8},{7,9},{8,10},{9,11},{10,... | collective-permute-start | bytes 688136 | tf_op jit(solution)/shard_map/ppermute | solution.py:247
  403.8 10.8 %collective-permute-start.29 = (bf16[64,1792]{1,0:T(8,128)(2,1)S(1)}, bf16[64,1792]{1,0:T(8,128)(2,1)S(1)}, u32[]{:S(2)}, u32[]{:S(2)}) collective-permute-start(bf16[64,1792]{1,0:T(8,128)(2,1)S(1)} %shard_map.89), channel_id=1, source_target_pairs={{0,62},{1,63},{2,0},{3,1},{4,2},{5,3},{6,4},{7,5},{8,6},{9,7},{10,... | collective-permute-start | bytes 688136 | tf_op jit(solution)/shard_map/ppermute | solution.py:247
  405.1 13.3 %collective-permute-start.44 = (bf16[64,1792]{1,0:T(8,128)(2,1)S(1)}, bf16[64,1792]{1,0:T(8,128)(2,1)S(1)}, u32[]{:S(2)}, u32[]{:S(2)}) collective-permute-start(bf16[64,1792]{1,0:T(8,128)(2,1)S(1)} %shard_map.110), channel_id=1, source_target_pairs={{0,2},{1,3},{2,4},{3,5},{4,6},{5,7},{6,8},{7,9},{8,10},{9,11},{10,... | collective-permute-start | bytes 688136 | tf_op jit(solution)/shard_map/ppermute | solution.py:247
  406.2 12.8 %collective-permute-start.14 = (bf16[64,1792]{1,0:T(8,128)(2,1)S(1)}, bf16[64,1792]{1,0:T(8,128)(2,1)S(1)}, u32[]{:S(2)}, u32[]{:S(2)}) collective-permute-start(bf16[64,1792]{1,0:T(8,128)(2,1)S(1)} %shard_map.75), channel_id=1, source_target_pairs={{0,2},{1,3},{2,4},{3,5},{4,6},{5,7},{6,8},{7,9},{8,10},{9,11},{10,... | collective-permute-start | bytes 688136 | tf_op jit(solution)/shard_map/ppermute | solution.py:247
  419.1 11.7 %collective-permute-start.15 = (bf16[64,1792]{1,0:T(8,128)(2,1)S(1)}, bf16[64,1792]{1,0:T(8,128)(2,1)S(1)}, u32[]{:S(2)}, u32[]{:S(2)}) collective-permute-start(bf16[64,1792]{1,0:T(8,128)(2,1)S(1)} %shard_map.76), channel_id=1, source_target_pairs={{0,2},{1,3},{2,4},{3,5},{4,6},{5,7},{6,8},{7,9},{8,10},{9,11},{10,... | collective-permute-start | bytes 688136 | tf_op jit(solution)/shard_map/ppermute | solution.py:247
  419.5 11.6 %collective-permute-start.61 = (bf16[64,1792]{1,0:T(8,128)(2,1)S(1)}, bf16[64,1792]{1,0:T(8,128)(2,1)S(1)}, u32[]{:S(2)}, u32[]{:S(2)}) collective-permute-start(bf16[64,1792]{1,0:T(8,128)(2,1)S(1)} %shard_map.126), channel_id=1, source_target_pairs={{0,62},{1,63},{2,0},{3,1},{4,2},{5,3},{6,4},{7,5},{8,6},{9,7},{10,... | collective-permute-start | bytes 688136 | tf_op jit(solution)/shard_map/ppermute | solution.py:247
  424.1 11.5 %collective-permute-start.31 = (bf16[64,1792]{1,0:T(8,128)(2,1)S(1)}, bf16[64,1792]{1,0:T(8,128)(2,1)S(1)}, u32[]{:S(2)}, u32[]{:S(2)}) collective-permute-start(bf16[64,1792]{1,0:T(8,128)(2,1)S(1)} %shard_map.91), channel_id=1, source_target_pairs={{0,62},{1,63},{2,0},{3,1},{4,2},{5,3},{6,4},{7,5},{8,6},{9,7},{10,... | collective-permute-start | bytes 688136 | tf_op jit(solution)/shard_map/ppermute | solution.py:247
  (16 other events, 136.1 us)

commit v2 on v1

--- a/solution.py
+++ b/solution.py
@@ -7,7 +7,7 @@
 
 CHAINS = 2
 STEPS = (4, 4, 4, 4)
-PIECES = (1, 2, 2, 2)
+PIECES = (1, 4, 4, 4)
 PARTS = 4
 INTERPRET = False
 
@@ -132,14 +132,23 @@
     )(target, gates, routed)
 
 
-def expert_kernel(place_ref, *refs, count, capacity):
+def expert_kernel(place_ref, *refs, count, capacity, start):
     packed = refs[:count]
-    own_weight, other_weight, out_ref = refs[count:]
-    tokens = out_ref.shape[1]
+    own_weight, other_weight, out_ref = refs[count : count + 3]
+    tokens, wide = out_ref.shape[1:]
     core = place_ref[1]
     tiles = own_weight.shape[0] // 128
-
-    def project(side, weight):
+    reads = {}
+    if start is not None:
+        buffers, arrive = refs[count + 3 : count + 5], refs[count + 5]
+        for i, (weight, buffer) in enumerate(zip((own_weight, other_weight), buffers)):
+            reads[i] = pltpu.make_async_copy(
+                weight.at[:, pl.ds(start, wide)], buffer, arrive.at[i]
+            )
+            reads[i].start()
+        own_weight, other_weight = buffers
+
+    def project(side, weight, read):
         blocks = [
             jnp.concatenate(
                 [
@@ -151,10 +160,12 @@
             for p in packed
         ]
         rows = jnp.concatenate(blocks, axis=0)
+        if read is not None:
+            read.wait()
         return jnp.dot(rows, weight[...], preferred_element_type=jnp.float32).astype(jnp.bfloat16)
 
-    own = project(core, own_weight)
-    other = project(1 - core, other_weight)
+    own = project(core, own_weight, reads.get(0))
+    other = project(1 - core, other_weight, reads.get(1))
     lower = jnp.where(core == 0, own, other)
     upper = jnp.where(core == 0, other, own)
     lanes = 4 * capacity
@@ -173,7 +184,7 @@
     chips, tall, _ = packed.shape
     width, columns = own_weight.shape
     columns = columns // parts
-    steps = 2 if parts == CHAINS else 1
+    steps = 4 if parts == 1 else 1
     piece = columns // steps
     count = len(homes)
 
@@ -182,16 +193,23 @@
             (1, tall, 128), lambda j, s: (lax.rem(s[0] + (home + chips), chips), 0, 0)
         )
 
-    weight_spec = pl.BlockSpec((width, piece), lambda j, s: (0, part * steps + j))
+    if steps > 1:
+        weight_spec = pl.BlockSpec((width, piece), lambda j, s: (0, j))
+        start, scratch = None, []
+    else:
+        weight_spec = pl.BlockSpec(memory_space=pltpu.HBM)
+        start = part * piece
+        scratch = [pltpu.VMEM((width, piece), jnp.bfloat16)] * 2 + [pltpu.SemaphoreType.DMA((2,))]
     grid_spec = pltpu.PrefetchScalarGridSpec(
         num_scalar_prefetch=1,
         grid=(steps,),
         in_specs=[row_spec(h) for h in homes] + [weight_spec] * 2,
         out_specs=pl.BlockSpec((count, tokens, piece), lambda j, s: (0, 0, j)),
+        scratch_shapes=scratch,
     )
     flops = 4 * count * capacity * width * columns
     return pl.pallas_call(
-        lambda *refs: expert_kernel(*refs, count=count, capacity=capacity),
+        lambda *refs: expert_kernel(*refs, count=count, capacity=capacity, start=start),
         grid_spec=grid_spec,
         out_shape=jax.ShapeDtypeStruct((count, tokens, columns), jnp.bfloat16),
         cost_estimate=pl.CostEstimate(
@@ -219,13 +237,14 @@
     lax.fori_loop(0, out_ref.shape[0] // 16, some, 0)
 
 
-def add_own(arrived, batches, place):
+def add_own(arrived, batches, place, at):
     whole = pl.BlockSpec(arrived.shape, lambda i: (0, 0))
+    block = (1, arrived.shape[0], arrived.shape[1] // len(batches))
     return pl.pallas_call(
         add_kernel,
         grid=(1,),
         in_specs=[whole]
-        + [pl.BlockSpec((1,) + batch.shape[1:], lambda i: (place, 0, 0)) for batch in batches],
+        + [pl.BlockSpec(block, lambda i: (place, 0, at)) for _ in batches],
         out_specs=whole,
         out_shape=jax.ShapeDtypeStruct(arrived.shape, jnp.bfloat16),
         compiler_params=pltpu.CompilerParams(vmem_limit_bytes=4 * 1024 * 1024),
@@ -276,28 +295,35 @@
         steps = range(first, first + count)
         first += count
         homes = [half - s for s in steps] + [s + 1 - half for s in steps]
-        for c in range(CHAINS):
-            batches = []
-            for piece in range(pieces):
-                batches.append(
-                    expert_call(
-                        place,
-                        packed,
-                        weight,
-                        other_weight,
-                        homes,
-                        tokens,
-                        capacity,
-                        c * pieces + piece,
-                        CHAINS * pieces,
-                    )
+        batches = []
+        for piece in range(pieces):
+            batches.append(
+                expert_call(
+                    place,
+                    packed,
+                    weight,
+                    other_weight,
+                    homes,
+                    tokens,
+                    capacity,
+                    piece,
+                    pieces,
                 )
-            for i, home in enumerate(homes):
-                sums[home, c] = (batches, i)
+            )
+        for i, home in enumerate(homes):
+            for c in range(CHAINS):
+                if pieces < CHAINS:
+                    sums[home, c] = (batches, i, c)
+                else:
+                    each = pieces // CHAINS
+                    sums[home, c] = (batches[c * each : (c + 1) * each], i, 0)
 
     def own_sum(home, c):
-        batches, i = sums[home, c]
-        return jnp.concatenate([batch[i] for batch in batches], axis=1)
+        batches, i, at = sums[home, c]
+        wide = weight.shape[1] // CHAINS // len(batches)
+        return jnp.concatenate(
+            [batch[i, :, at * wide : (at + 1) * wide] for batch in batches], axis=1
+        )
 
     def with_own(arrived, home, c):
         return add_own(arrived, *sums[home, c])

time: 453 us -> 449 us (level)
    pallas_call x14 -> x13, Pallas kernels: 54 us -> 49.3 us  [expert_call(): pl.pallas_call(lambda *refs: expert_kernel(*refs, count=count, capacity=c...]
  transfers between devices with their start and end apart: 64 -> 64, of which waited for: 25 -> 22; matrix products, arithmetic and copies ran while one was open for 0% -> 0% of each run, Pallas kernels for 12% -> 10%
where the time goes in v2:
time: 449 us; the launch traced here: 440 us
  waiting for transfers between devices  246 us (55%)
  starting transfers between devices  130 us (29%)
  Pallas kernels  58.2 us (13%)
    all_to_all x1, waiting for transfers between devices, on_device(): lax.all_to_all(packed, 'ep', split_axis=0, concat_axis=0, axis_index_grou...  190 us
    ppermute x62, starting transfers between devices, shifted(): lax.ppermute(value, 'ep', [(i, (i + 2 * distance) % experts) for i in ran...  97.6 us
    pallas_call x13, Pallas kernels, expert_call(): pl.pallas_call(lambda *refs: expert_kernel(*refs, count=count, capacity=c...  49.3 us
    ppermute x62, waiting for transfers between devices, shifted(): lax.ppermute(value, 'ep', [(i, (i + 2 * distance) % experts) for i in ran...  44 us
    all_to_all x1, starting transfers between devices, on_device(): lax.all_to_all(packed, 'ep', split_axis=0, concat_axis=0, axis_index_grou...  32.7 us
    ppermute x1, waiting for transfers between devices, on_device(): lax.ppermute(weight, 'ep', [(i, i ^ 1) for i in range(experts)])  11.9 us
  transfers between devices with their start and end apart: 64, of which 22 were waited for; matrix products, arithmetic and copies ran while one was open for 0% of the time, Pallas kernels for 10%

profile of v2, /device:TPU:46, one launch (start us, length us, event | category | flops | bytes accessed | tf_op | source)
XLA Modules:
  0.0 439.9 jit_solution(13432245873093660000)
XLA Ops:
  3.6 4.4 %shard_map.55 = bf16[32,264,128]{2,1,0:T(8,128)(2,1)} custom-call(s32[1,512]{1,0:T(1,128)} %reshape.9.refs_0_, f32[1,512]{1,0:T(1,128)} %reshape.10.refs_1_, bf16[512,2048]{1,0:T(8,128)(2,1)} %bitcast.36), custom_call_target="tpu_custom_call" | custom-call | tf_op jit(solution)/shard_map/pallas_call | solution.py:113
  8.0 32.7 %all-to-all-start = ((bf16[32,264,128]{2,1,0:T(8,128)(2,1)}), bf16[32,264,128]{2,1,0:T(8,128)(2,1)S(1)}, u32[]{:S(2)}, u32[]{:S(2)}) async-start(bf16[32,264,128]{2,1,0:T(8,128)(2,1)} %shard_map.55), calls=%async_computation | async-start | bytes 4325376 | tf_op jit(solution)/shard_map/all_to_all | solution.py:281
  40.9 11.9 %collective-permute-done.refs_10_ = bf16[1024,3584]{1,0:T(8,128)(2,1)} collective-permute-done((bf16[1024,3584]{1,0:T(8,128)(2,1)}, bf16[1024,3584]{1,0:T(8,128)(2,1)}, u32[]{:S(2)}, u32[]{:S(2)}) %collective-permute-start) | collective-permute-done | bytes 7340064 | tf_op jit(solution)/shard_map/ppermute | solution.py:280
  52.8 189.7 %all-to-all-done.refs_1_.refs_2_.refs_3_.refs_4_.refs_5_.refs_6_.refs_7_.refs_8_ = bf16[32,264,128]{2,1,0:T(8,128)(2,1)S(1)} async-done(((bf16[32,264,128]{2,1,0:T(8,128)(2,1)}), bf16[32,264,128]{2,1,0:T(8,128)(2,1)S(1)}, u32[]{:S(2)}, u32[]{:S(2)}) %all-to-all-start) | async-done | bytes 2162720 | tf_op jit(solution)/shard_map/all_to_all | solution.py:281
  242.5 8.3 %shard_map.56.refs_0_ = bf16[8,64,3584]{2,1,0:T(8,128)(2,1)S(1)} custom-call(s32[2]{0:T(128)S(1)} %pad_add_fusion.refs_0_, bf16[32,264,128]{2,1,0:T(8,128)(2,1)S(1)} %all-to-all-done.refs_1_.refs_2_.refs_3_.refs_4_.refs_5_.refs_6_.refs_7_.refs_8_, bf16[32,264,128]{2,1,0:T(8,128)(2,1)S(1)} %all-to-all-done.refs_1_.refs_2_.refs_3_.refs_4_.refs_5_.refs_6_.refs_7_.refs_8_, ...), custom_call_target="tpu_custom_call" | custom-call | flops 1879048192 | bytes 14680064 | tf_op jit(solution)/shard_map/pallas_call | solution.py:211
  251.1 3.2 collective-permute-start.17
  254.3 4.0 collective-permute-done.1.left_ref
  259.4 2.3 collective-permute-start.48
  264.2 4.1 collective-permute-done.2.left_ref
  268.6 3.8 collective-permute-start.49
  274.8 3.1 collective-permute-done.3.left_ref
  278.2 3.4 shard_map.60.refs_0_
  281.6 3.4 shard_map.61.refs_1_
  285.1 3.3 collective-permute-start.50
  291.1 3.4 shard_map.95.refs_0_
  294.5 3.4 shard_map.96.refs_1_
  298.1 3.3 collective-permute-start.51
  304.2 3.1 collective-permute-done.51.left_ref
  307.3 3.8 collective-permute-start.52
  312.3 3.8 collective-permute-start.22
  317.4 3.6 collective-permute-start.53
  322.1 3.8 collective-permute-start.23
  326.2 3.7 collective-permute-done.7.left_ref
  330.1 3.4 shard_map.66.refs_0_
  333.5 3.4 shard_map.67.refs_1_
  337.0 3.3 collective-permute-start.54
  343.2 3.4 shard_map.101.refs_0_
  346.6 3.4 shard_map.102.refs_1_
  350.2 3.3 collective-permute-start.55
  356.1 2.5 collective-permute-done.55.left_ref
  358.6 3.8 collective-permute-start.56
  363.6 3.8 collective-permute-start.26
  368.5 3.3 collective-permute-start.57
  372.1 4.2 collective-permute-start.27
  376.5 4.3 collective-permute-done.11.left_ref
  381.1 3.4 shard_map.72.refs_0_
  384.5 3.4 shard_map.73.refs_1_
  388.0 3.3 collective-permute-start.58
  394.0 3.4 shard_map.107.refs_0_
  397.4 3.4 shard_map.108.refs_1_
  400.9 3.3 collective-permute-start.59
  407.0 2.5 collective-permute-done.59.left_ref
  409.6 3.8 collective-permute-start.60
  413.5 3.1 collective-permute-start.30
  417.7 3.1 collective-permute-start.61
  420.9 3.1 collective-permute-start.31
  426.8 3.3 collective-permute-start.62
  434.0 4.9 %collective-permute-done.47 = bf16[64,1792]{1,0:T(8,128)(2,1)S(1)} collective-permute-done((bf16[64,1792]{1,0:T(8,128)(2,1)S(1)}, bf16[64,1792]{1,0:T(8,128)(2,1)S(1)}, u32[]{:S(2)}, u32[]{:S(2)}) %collective-permute-start.47) | collective-permute-done | bytes 229408 | tf_op jit(solution)/shard_map/ppermute | solution.py:266
  (164 shorter events, 42.5 us)
Async XLA Ops:
  8.0 234.5 %all-to-all-start = ((bf16[32,264,128]{2,1,0:T(8,128)(2,1)}), bf16[32,264,128]{2,1,0:T(8,128)(2,1)S(1)}, u32[]{:S(2)}, u32[]{:S(2)}) async-start(bf16[32,264,128]{2,1,0:T(8,128)(2,1)} %shard_map.55), calls=%async_computation | async-start | bytes 4325376 | tf_op jit(solution)/shard_map/all_to_all | solution.py:281
  40.7 12.1 %collective-permute-start = (bf16[1024,3584]{1,0:T(8,128)(2,1)}, bf16[1024,3584]{1,0:T(8,128)(2,1)}, u32[]{:S(2)}, u32[]{:S(2)}) collective-permute-start(bf16[1024,3584]{1,0:T(8,128)(2,1)} %bitcast.22), channel_id=1, source_target_pairs={{0,1},{1,0},{2,3},{3,2},{4,5},{5,4},{6,7},{7,6},{8,9},{9,8},{10,11... | collective-permute-start | bytes 22020104 | tf_op jit(solution)/shard_map/ppermute | solution.py:280
  251.1 10.7 %collective-permute-start.17 = (bf16[64,1792]{1,0:T(8,128)(2,1)S(1)}, bf16[64,1792]{1,0:T(8,128)(2,1)S(1)}, u32[]{:S(2)}, u32[]{:S(2)}) collective-permute-start(bf16[64,1792]{1,0:T(8,128)(2,1)S(1)} %get-tuple-element.8), channel_id=1, source_target_pairs={{0,62},{1,63},{2,0},{3,1},{4,2},{5,3},{6,4},{7,5},{8,6},{9,7},{10,... | collective-permute-start | bytes 688136 | tf_op jit(solution)/shard_map/ppermute | solution.py:266
  258.4 9.9 %collective-permute-start.2 = (bf16[64,1792]{1,0:T(8,128)(2,1)S(1)}, bf16[64,1792]{1,0:T(8,128)(2,1)S(1)}, u32[]{:S(2)}, u32[]{:S(2)}) collective-permute-start(bf16[64,1792]{1,0:T(8,128)(2,1)S(1)} %shard_map.57), channel_id=1, source_target_pairs={{0,2},{1,3},{2,4},{3,5},{4,6},{5,7},{6,8},{7,9},{8,10},{9,11},{10,... | collective-permute-start | bytes 688136 | tf_op jit(solution)/shard_map/ppermute | solution.py:266
  261.8 10.6 %collective-permute-start.18 = (bf16[64,1792]{1,0:T(8,128)(2,1)S(1)}, bf16[64,1792]{1,0:T(8,128)(2,1)S(1)}, u32[]{:S(2)}, u32[]{:S(2)}) collective-permute-start(bf16[64,1792]{1,0:T(8,128)(2,1)S(1)} %shard_map.78), channel_id=1, source_target_pairs={{0,62},{1,63},{2,0},{3,1},{4,2},{5,3},{6,4},{7,5},{8,6},{9,7},{10,... | collective-permute-start | bytes 688136 | tf_op jit(solution)/shard_map/ppermute | solution.py:266
  263.4 9.7 %collective-permute-start.33 = (bf16[64,1792]{1,0:T(8,128)(2,1)S(1)}, bf16[64,1792]{1,0:T(8,128)(2,1)S(1)}, u32[]{:S(2)}, u32[]{:S(2)}) collective-permute-start(bf16[64,1792]{1,0:T(8,128)(2,1)S(1)} %shard_map.92), channel_id=1, source_target_pairs={{0,2},{1,3},{2,4},{3,5},{4,6},{5,7},{6,8},{7,9},{8,10},{9,11},{10,... | collective-permute-start | bytes 688136 | tf_op jit(solution)/shard_map/ppermute | solution.py:266
  268.4 9.6 %collective-permute-start.3 = (bf16[64,1792]{1,0:T(8,128)(2,1)S(1)}, bf16[64,1792]{1,0:T(8,128)(2,1)S(1)}, u32[]{:S(2)}, u32[]{:S(2)}) collective-permute-start(bf16[64,1792]{1,0:T(8,128)(2,1)S(1)} %shard_map.58), channel_id=1, source_target_pairs={{0,2},{1,3},{2,4},{3,5},{4,6},{5,7},{6,8},{7,9},{8,10},{9,11},{10,... | collective-permute-start | bytes 688136 | tf_op jit(solution)/shard_map/ppermute | solution.py:266
  268.6 16.4 %collective-permute-start.49 = (bf16[64,1792]{1,0:T(8,128)(2,1)S(1)}, bf16[64,1792]{1,0:T(8,128)(2,1)S(1)}, u32[]{:S(2)}, u32[]{:S(2)}) collective-permute-start(bf16[64,1792]{1,0:T(8,128)(2,1)S(1)} %shard_map.113), channel_id=1, source_target_pairs={{0,62},{1,63},{2,0},{3,1},{4,2},{5,3},{6,4},{7,5},{8,6},{9,7},{10,... | collective-permute-start | bytes 688136 | tf_op jit(solution)/shard_map/ppermute | solution.py:266
  272.5 15.9 %collective-permute-start.19 = (bf16[64,1792]{1,0:T(8,128)(2,1)S(1)}, bf16[64,1792]{1,0:T(8,128)(2,1)S(1)}, u32[]{:S(2)}, u32[]{:S(2)}) collective-permute-start(bf16[64,1792]{1,0:T(8,128)(2,1)S(1)} %shard_map.79), channel_id=1, source_target_pairs={{0,62},{1,63},{2,0},{3,1},{4,2},{5,3},{6,4},{7,5},{8,6},{9,7},{10,... | collective-permute-start | bytes 688136 | tf_op jit(solution)/shard_map/ppermute | solution.py:266
  273.3 15.4 %collective-permute-start.34 = (bf16[64,1792]{1,0:T(8,128)(2,1)S(1)}, bf16[64,1792]{1,0:T(8,128)(2,1)S(1)}, u32[]{:S(2)}, u32[]{:S(2)}) collective-permute-start(bf16[64,1792]{1,0:T(8,128)(2,1)S(1)} %shard_map.93), channel_id=1, source_target_pairs={{0,2},{1,3},{2,4},{3,5},{4,6},{5,7},{6,8},{7,9},{8,10},{9,11},{10,... | collective-permute-start | bytes 688136 | tf_op jit(solution)/shard_map/ppermute | solution.py:266
  278.0 12.9 %collective-permute-start.4 = (bf16[64,1792]{1,0:T(8,128)(2,1)S(1)}, bf16[64,1792]{1,0:T(8,128)(2,1)S(1)}, u32[]{:S(2)}, u32[]{:S(2)}) collective-permute-start(bf16[64,1792]{1,0:T(8,128)(2,1)S(1)} %shard_map.59), channel_id=1, source_target_pairs={{0,2},{1,3},{2,4},{3,5},{4,6},{5,7},{6,8},{7,9},{8,10},{9,11},{10,... | collective-permute-start | bytes 688136 | tf_op jit(solution)/shard_map/ppermute | solution.py:266
  285.1 12.8 %collective-permute-start.50 = (bf16[64,1792]{1,0:T(8,128)(2,1)S(1)}, bf16[64,1792]{1,0:T(8,128)(2,1)S(1)}, u32[]{:S(2)}, u32[]{:S(2)}) collective-permute-start(bf16[64,1792]{1,0:T(8,128)(2,1)S(1)} %shard_map.114), channel_id=1, source_target_pairs={{0,62},{1,63},{2,0},{3,1},{4,2},{5,3},{6,4},{7,5},{8,6},{9,7},{10,... | collective-permute-start | bytes 688136 | tf_op jit(solution)/shard_map/ppermute | solution.py:266
  288.5 12.8 %collective-permute-start.20 = (bf16[64,1792]{1,0:T(8,128)(2,1)S(1)}, bf16[64,1792]{1,0:T(8,128)(2,1)S(1)}, u32[]{:S(2)}, u32[]{:S(2)}) collective-permute-start(bf16[64,1792]{1,0:T(8,128)(2,1)S(1)} %shard_map.80), channel_id=1, source_target_pairs={{0,62},{1,63},{2,0},{3,1},{4,2},{5,3},{6,4},{7,5},{8,6},{9,7},{10,... | collective-permute-start | bytes 688136 | tf_op jit(solution)/shard_map/ppermute | solution.py:266
  288.8 13.0 %collective-permute-start.35 = (bf16[64,1792]{1,0:T(8,128)(2,1)S(1)}, bf16[64,1792]{1,0:T(8,128)(2,1)S(1)}, u32[]{:S(2)}, u32[]{:S(2)}) collective-permute-start(bf16[64,1792]{1,0:T(8,128)(2,1)S(1)} %shard_map.94), channel_id=1, source_target_pairs={{0,2},{1,3},{2,4},{3,5},{4,6},{5,7},{6,8},{7,9},{8,10},{9,11},{10,... | collective-permute-start | bytes 688136 | tf_op jit(solution)/shard_map/ppermute | solution.py:266
  291.0 13.0 %collective-permute-start.5 = (bf16[64,1792]{1,0:T(8,128)(2,1)S(1)}, bf16[64,1792]{1,0:T(8,128)(2,1)S(1)}, u32[]{:S(2)}, u32[]{:S(2)}) collective-permute-start(bf16[64,1792]{1,0:T(8,128)(2,1)S(1)} %shard_map.62), channel_id=1, source_target_pairs={{0,2},{1,3},{2,4},{3,5},{4,6},{5,7},{6,8},{7,9},{8,10},{9,11},{10,... | collective-permute-start | bytes 688136 | tf_op jit(solution)/shard_map/ppermute | solution.py:266
  298.1 9.2 %collective-permute-start.51 = (bf16[64,1792]{1,0:T(8,128)(2,1)S(1)}, bf16[64,1792]{1,0:T(8,128)(2,1)S(1)}, u32[]{:S(2)}, u32[]{:S(2)}) collective-permute-start(bf16[64,1792]{1,0:T(8,128)(2,1)S(1)} %shard_map.115), channel_id=1, source_target_pairs={{0,62},{1,63},{2,0},{3,1},{4,2},{5,3},{6,4},{7,5},{8,6},{9,7},{10,... | collective-permute-start | bytes 688136 | tf_op jit(solution)/shard_map/ppermute | solution.py:266
  301.4 10.7 %collective-permute-start.21 = (bf16[64,1792]{1,0:T(8,128)(2,1)S(1)}, bf16[64,1792]{1,0:T(8,128)(2,1)S(1)}, u32[]{:S(2)}, u32[]{:S(2)}) collective-permute-start(bf16[64,1792]{1,0:T(8,128)(2,1)S(1)} %shard_map.81), channel_id=1, source_target_pairs={{0,62},{1,63},{2,0},{3,1},{4,2},{5,3},{6,4},{7,5},{8,6},{9,7},{10,... | collective-permute-start | bytes 688136 | tf_op jit(solution)/shard_map/ppermute | solution.py:266
  301.9 14.2 %collective-permute-start.36 = (bf16[64,1792]{1,0:T(8,128)(2,1)S(1)}, bf16[64,1792]{1,0:T(8,128)(2,1)S(1)}, u32[]{:S(2)}, u32[]{:S(2)}) collective-permute-start(bf16[64,1792]{1,0:T(8,128)(2,1)S(1)} %shard_map.97), channel_id=1, source_target_pairs={{0,2},{1,3},{2,4},{3,5},{4,6},{5,7},{6,8},{7,9},{8,10},{9,11},{10,... | collective-permute-start | bytes 688136 | tf_op jit(solution)/shard_map/ppermute | solution.py:266
  304.0 12.3 %collective-permute-start.6 = (bf16[64,1792]{1,0:T(8,128)(2,1)S(1)}, bf16[64,1792]{1,0:T(8,128)(2,1)S(1)}, u32[]{:S(2)}, u32[]{:S(2)}) collective-permute-start(bf16[64,1792]{1,0:T(8,128)(2,1)S(1)} %shard_map.63), channel_id=1, source_target_pairs={{0,2},{1,3},{2,4},{3,5},{4,6},{5,7},{6,8},{7,9},{8,10},{9,11},{10,... | collective-permute-start | bytes 688136 | tf_op jit(solution)/shard_map/ppermute | solution.py:266
  307.3 10.0 %collective-permute-start.52 = (bf16[64,1792]{1,0:T(8,128)(2,1)S(1)}, bf16[64,1792]{1,0:T(8,128)(2,1)S(1)}, u32[]{:S(2)}, u32[]{:S(2)}) collective-permute-start(bf16[64,1792]{1,0:T(8,128)(2,1)S(1)} %shard_map.116), channel_id=1, source_target_pairs={{0,62},{1,63},{2,0},{3,1},{4,2},{5,3},{6,4},{7,5},{8,6},{9,7},{10,... | collective-permute-start | bytes 688136 | tf_op jit(solution)/shard_map/ppermute | solution.py:266
  312.3 9.8 %collective-permute-start.22 = (bf16[64,1792]{1,0:T(8,128)(2,1)S(1)}, bf16[64,1792]{1,0:T(8,128)(2,1)S(1)}, u32[]{:S(2)}, u32[]{:S(2)}) collective-permute-start(bf16[64,1792]{1,0:T(8,128)(2,1)S(1)} %shard_map.82), channel_id=1, source_target_pairs={{0,62},{1,63},{2,0},{3,1},{4,2},{5,3},{6,4},{7,5},{8,6},{9,7},{10,... | collective-permute-start | bytes 688136 | tf_op jit(solution)/shard_map/ppermute | solution.py:266
  316.1 9.8 %collective-permute-start.37 = (bf16[64,1792]{1,0:T(8,128)(2,1)S(1)}, bf16[64,1792]{1,0:T(8,128)(2,1)S(1)}, u32[]{:S(2)}, u32[]{:S(2)}) collective-permute-start(bf16[64,1792]{1,0:T(8,128)(2,1)S(1)} %shard_map.98), channel_id=1, source_target_pairs={{0,2},{1,3},{2,4},{3,5},{4,6},{5,7},{6,8},{7,9},{8,10},{9,11},{10,... | collective-permute-start | bytes 688136 | tf_op jit(solution)/shard_map/ppermute | solution.py:266
  316.4 13.5 %collective-permute-start.7 = (bf16[64,1792]{1,0:T(8,128)(2,1)S(1)}, bf16[64,1792]{1,0:T(8,128)(2,1)S(1)}, u32[]{:S(2)}, u32[]{:S(2)}) collective-permute-start(bf16[64,1792]{1,0:T(8,128)(2,1)S(1)} %shard_map.64), channel_id=1, source_target_pairs={{0,2},{1,3},{2,4},{3,5},{4,6},{5,7},{6,8},{7,9},{8,10},{9,11},{10,... | collective-permute-start | bytes 688136 | tf_op jit(solution)/shard_map/ppermute | solution.py:266
  317.4 19.5 %collective-permute-start.53 = (bf16[64,1792]{1,0:T(8,128)(2,1)S(1)}, bf16[64,1792]{1,0:T(8,128)(2,1)S(1)}, u32[]{:S(2)}, u32[]{:S(2)}) collective-permute-start(bf16[64,1792]{1,0:T(8,128)(2,1)S(1)} %shard_map.117), channel_id=1, source_target_pairs={{0,62},{1,63},{2,0},{3,1},{4,2},{5,3},{6,4},{7,5},{8,6},{9,7},{10,... | collective-permute-start | bytes 688136 | tf_op jit(solution)/shard_map/ppermute | solution.py:266
  322.1 18.2 %collective-permute-start.23 = (bf16[64,1792]{1,0:T(8,128)(2,1)S(1)}, bf16[64,1792]{1,0:T(8,128)(2,1)S(1)}, u32[]{:S(2)}, u32[]{:S(2)}) collective-permute-start(bf16[64,1792]{1,0:T(8,128)(2,1)S(1)} %shard_map.83), channel_id=1, source_target_pairs={{0,62},{1,63},{2,0},{3,1},{4,2},{5,3},{6,4},{7,5},{8,6},{9,7},{10,... | collective-permute-start | bytes 688136 | tf_op jit(solution)/shard_map/ppermute | solution.py:266
  326.0 14.8 %collective-permute-start.38 = (bf16[64,1792]{1,0:T(8,128)(2,1)S(1)}, bf16[64,1792]{1,0:T(8,128)(2,1)S(1)}, u32[]{:S(2)}, u32[]{:S(2)}) collective-permute-start(bf16[64,1792]{1,0:T(8,128)(2,1)S(1)} %shard_map.99), channel_id=1, source_target_pairs={{0,2},{1,3},{2,4},{3,5},{4,6},{5,7},{6,8},{7,9},{8,10},{9,11},{10,... | collective-permute-start | bytes 688136 | tf_op jit(solution)/shard_map/ppermute | solution.py:266
  329.9 13.0 %collective-permute-start.8 = (bf16[64,1792]{1,0:T(8,128)(2,1)S(1)}, bf16[64,1792]{1,0:T(8,128)(2,1)S(1)}, u32[]{:S(2)}, u32[]{:S(2)}) collective-permute-start(bf16[64,1792]{1,0:T(8,128)(2,1)S(1)} %shard_map.65), channel_id=1, source_target_pairs={{0,2},{1,3},{2,4},{3,5},{4,6},{5,7},{6,8},{7,9},{8,10},{9,11},{10,... | collective-permute-start | bytes 688136 | tf_op jit(solution)/shard_map/ppermute | solution.py:266
  337.0 13.0 %collective-permute-start.54 = (bf16[64,1792]{1,0:T(8,128)(2,1)S(1)}, bf16[64,1792]{1,0:T(8,128)(2,1)S(1)}, u32[]{:S(2)}, u32[]{:S(2)}) collective-permute-start(bf16[64,1792]{1,0:T(8,128)(2,1)S(1)} %shard_map.118), channel_id=1, source_target_pairs={{0,62},{1,63},{2,0},{3,1},{4,2},{5,3},{6,4},{7,5},{8,6},{9,7},{10,... | collective-permute-start | bytes 688136 | tf_op jit(solution)/shard_map/ppermute | solution.py:266
  340.4 13.0 %collective-permute-start.24 = (bf16[64,1792]{1,0:T(8,128)(2,1)S(1)}, bf16[64,1792]{1,0:T(8,128)(2,1)S(1)}, u32[]{:S(2)}, u32[]{:S(2)}) collective-permute-start(bf16[64,1792]{1,0:T(8,128)(2,1)S(1)} %shard_map.84), channel_id=1, source_target_pairs={{0,62},{1,63},{2,0},{3,1},{4,2},{5,3},{6,4},{7,5},{8,6},{9,7},{10,... | collective-permute-start | bytes 688136 | tf_op jit(solution)/shard_map/ppermute | solution.py:266
  340.9 14.3 %collective-permute-start.39 = (bf16[64,1792]{1,0:T(8,128)(2,1)S(1)}, bf16[64,1792]{1,0:T(8,128)(2,1)S(1)}, u32[]{:S(2)}, u32[]{:S(2)}) collective-permute-start(bf16[64,1792]{1,0:T(8,128)(2,1)S(1)} %shard_map.100), channel_id=1, source_target_pairs={{0,2},{1,3},{2,4},{3,5},{4,6},{5,7},{6,8},{7,9},{8,10},{9,11},{10,... | collective-permute-start | bytes 688136 | tf_op jit(solution)/shard_map/ppermute | solution.py:266
  343.1 12.8 %collective-permute-start.9 = (bf16[64,1792]{1,0:T(8,128)(2,1)S(1)}, bf16[64,1792]{1,0:T(8,128)(2,1)S(1)}, u32[]{:S(2)}, u32[]{:S(2)}) collective-permute-start(bf16[64,1792]{1,0:T(8,128)(2,1)S(1)} %shard_map.68), channel_id=1, source_target_pairs={{0,2},{1,3},{2,4},{3,5},{4,6},{5,7},{6,8},{7,9},{8,10},{9,11},{10,... | collective-permute-start | bytes 688136 | tf_op jit(solution)/shard_map/ppermute | solution.py:266
  353.5 9.9 %collective-permute-start.25 = (bf16[64,1792]{1,0:T(8,128)(2,1)S(1)}, bf16[64,1792]{1,0:T(8,128)(2,1)S(1)}, u32[]{:S(2)}, u32[]{:S(2)}) collective-permute-start(bf16[64,1792]{1,0:T(8,128)(2,1)S(1)} %shard_map.85), channel_id=1, source_target_pairs={{0,62},{1,63},{2,0},{3,1},{4,2},{5,3},{6,4},{7,5},{8,6},{9,7},{10,... | collective-permute-start | bytes 688136 | tf_op jit(solution)/shard_map/ppermute | solution.py:266
  355.2 12.1 %collective-permute-start.40 = (bf16[64,1792]{1,0:T(8,128)(2,1)S(1)}, bf16[64,1792]{1,0:T(8,128)(2,1)S(1)}, u32[]{:S(2)}, u32[]{:S(2)}) collective-permute-start(bf16[64,1792]{1,0:T(8,128)(2,1)S(1)} %shard_map.103), channel_id=1, source_target_pairs={{0,2},{1,3},{2,4},{3,5},{4,6},{5,7},{6,8},{7,9},{8,10},{9,11},{10,... | collective-permute-start | bytes 688136 | tf_op jit(solution)/shard_map/ppermute | solution.py:266
  355.9 12.2 %collective-permute-start.10 = (bf16[64,1792]{1,0:T(8,128)(2,1)S(1)}, bf16[64,1792]{1,0:T(8,128)(2,1)S(1)}, u32[]{:S(2)}, u32[]{:S(2)}) collective-permute-start(bf16[64,1792]{1,0:T(8,128)(2,1)S(1)} %shard_map.69), channel_id=1, source_target_pairs={{0,2},{1,3},{2,4},{3,5},{4,6},{5,7},{6,8},{7,9},{8,10},{9,11},{10,... | collective-permute-start | bytes 688136 | tf_op jit(solution)/shard_map/ppermute | solution.py:266
  358.6 9.7 %collective-permute-start.56 = (bf16[64,1792]{1,0:T(8,128)(2,1)S(1)}, bf16[64,1792]{1,0:T(8,128)(2,1)S(1)}, u32[]{:S(2)}, u32[]{:S(2)}) collective-permute-start(bf16[64,1792]{1,0:T(8,128)(2,1)S(1)} %shard_map.120), channel_id=1, source_target_pairs={{0,62},{1,63},{2,0},{3,1},{4,2},{5,3},{6,4},{7,5},{8,6},{9,7},{10,... | collective-permute-start | bytes 688136 | tf_op jit(solution)/shard_map/ppermute | solution.py:266
  368.2 12.6 %collective-permute-start.11 = (bf16[64,1792]{1,0:T(8,128)(2,1)S(1)}, bf16[64,1792]{1,0:T(8,128)(2,1)S(1)}, u32[]{:S(2)}, u32[]{:S(2)}) collective-permute-start(bf16[64,1792]{1,0:T(8,128)(2,1)S(1)} %shard_map.70), channel_id=1, source_target_pairs={{0,2},{1,3},{2,4},{3,5},{4,6},{5,7},{6,8},{7,9},{8,10},{9,11},{10,... | collective-permute-start | bytes 688136 | tf_op jit(solution)/shard_map/ppermute | solution.py:266
  368.5 19.4 %collective-permute-start.57 = (bf16[64,1792]{1,0:T(8,128)(2,1)S(1)}, bf16[64,1792]{1,0:T(8,128)(2,1)S(1)}, u32[]{:S(2)}, u32[]{:S(2)}) collective-permute-start(bf16[64,1792]{1,0:T(8,128)(2,1)S(1)} %shard_map.121), channel_id=1, source_target_pairs={{0,62},{1,63},{2,0},{3,1},{4,2},{5,3},{6,4},{7,5},{8,6},{9,7},{10,... | collective-permute-start | bytes 688136 | tf_op jit(solution)/shard_map/ppermute | solution.py:266
  372.1 19.2 %collective-permute-start.27 = (bf16[64,1792]{1,0:T(8,128)(2,1)S(1)}, bf16[64,1792]{1,0:T(8,128)(2,1)S(1)}, u32[]{:S(2)}, u32[]{:S(2)}) collective-permute-start(bf16[64,1792]{1,0:T(8,128)(2,1)S(1)} %shard_map.87), channel_id=1, source_target_pairs={{0,62},{1,63},{2,0},{3,1},{4,2},{5,3},{6,4},{7,5},{8,6},{9,7},{10,... | collective-permute-start | bytes 688136 | tf_op jit(solution)/shard_map/ppermute | solution.py:266
  376.4 15.2 %collective-permute-start.42 = (bf16[64,1792]{1,0:T(8,128)(2,1)S(1)}, bf16[64,1792]{1,0:T(8,128)(2,1)S(1)}, u32[]{:S(2)}, u32[]{:S(2)}) collective-permute-start(bf16[64,1792]{1,0:T(8,128)(2,1)S(1)} %shard_map.105), channel_id=1, source_target_pairs={{0,2},{1,3},{2,4},{3,5},{4,6},{5,7},{6,8},{7,9},{8,10},{9,11},{10,... | collective-permute-start | bytes 688136 | tf_op jit(solution)/shard_map/ppermute | solution.py:266
  380.9 12.8 %collective-permute-start.12 = (bf16[64,1792]{1,0:T(8,128)(2,1)S(1)}, bf16[64,1792]{1,0:T(8,128)(2,1)S(1)}, u32[]{:S(2)}, u32[]{:S(2)}) collective-permute-start(bf16[64,1792]{1,0:T(8,128)(2,1)S(1)} %shard_map.71), channel_id=1, source_target_pairs={{0,2},{1,3},{2,4},{3,5},{4,6},{5,7},{6,8},{7,9},{8,10},{9,11},{10,... | collective-permute-start | bytes 688136 | tf_op jit(solution)/shard_map/ppermute | solution.py:266
  388.0 12.8 %collective-permute-start.58 = (bf16[64,1792]{1,0:T(8,128)(2,1)S(1)}, bf16[64,1792]{1,0:T(8,128)(2,1)S(1)}, u32[]{:S(2)}, u32[]{:S(2)}) collective-permute-start(bf16[64,1792]{1,0:T(8,128)(2,1)S(1)} %shard_map.122), channel_id=1, source_target_pairs={{0,62},{1,63},{2,0},{3,1},{4,2},{5,3},{6,4},{7,5},{8,6},{9,7},{10,... | collective-permute-start | bytes 688136 | tf_op jit(solution)/shard_map/ppermute | solution.py:266
  391.4 12.8 %collective-permute-start.28 = (bf16[64,1792]{1,0:T(8,128)(2,1)S(1)}, bf16[64,1792]{1,0:T(8,128)(2,1)S(1)}, u32[]{:S(2)}, u32[]{:S(2)}) collective-permute-start(bf16[64,1792]{1,0:T(8,128)(2,1)S(1)} %shard_map.88), channel_id=1, source_target_pairs={{0,62},{1,63},{2,0},{3,1},{4,2},{5,3},{6,4},{7,5},{8,6},{9,7},{10,... | collective-permute-start | bytes 688136 | tf_op jit(solution)/shard_map/ppermute | solution.py:266
  391.6 12.8 %collective-permute-start.43 = (bf16[64,1792]{1,0:T(8,128)(2,1)S(1)}, bf16[64,1792]{1,0:T(8,128)(2,1)S(1)}, u32[]{:S(2)}, u32[]{:S(2)}) collective-permute-start(bf16[64,1792]{1,0:T(8,128)(2,1)S(1)} %shard_map.106), channel_id=1, source_target_pairs={{0,2},{1,3},{2,4},{3,5},{4,6},{5,7},{6,8},{7,9},{8,10},{9,11},{10,... | collective-permute-start | bytes 688136 | tf_op jit(solution)/shard_map/ppermute | solution.py:266
  393.8 13.0 %collective-permute-start.13 = (bf16[64,1792]{1,0:T(8,128)(2,1)S(1)}, bf16[64,1792]{1,0:T(8,128)(2,1)S(1)}, u32[]{:S(2)}, u32[]{:S(2)}) collective-permute-start(bf16[64,1792]{1,0:T(8,128)(2,1)S(1)} %shard_map.74), channel_id=1, source_target_pairs={{0,2},{1,3},{2,4},{3,5},{4,6},{5,7},{6,8},{7,9},{8,10},{9,11},{10,... | collective-permute-start | bytes 688136 | tf_op jit(solution)/shard_map/ppermute | solution.py:266
  404.5 12.0 %collective-permute-start.44 = (bf16[64,1792]{1,0:T(8,128)(2,1)S(1)}, bf16[64,1792]{1,0:T(8,128)(2,1)S(1)}, u32[]{:S(2)}, u32[]{:S(2)}) collective-permute-start(bf16[64,1792]{1,0:T(8,128)(2,1)S(1)} %shard_map.109), channel_id=1, source_target_pairs={{0,2},{1,3},{2,4},{3,5},{4,6},{5,7},{6,8},{7,9},{8,10},{9,11},{10,... | collective-permute-start | bytes 688136 | tf_op jit(solution)/shard_map/ppermute | solution.py:266
  406.9 10.1 %collective-permute-start.14 = (bf16[64,1792]{1,0:T(8,128)(2,1)S(1)}, bf16[64,1792]{1,0:T(8,128)(2,1)S(1)}, u32[]{:S(2)}, u32[]{:S(2)}) collective-permute-start(bf16[64,1792]{1,0:T(8,128)(2,1)S(1)} %shard_map.75), channel_id=1, source_target_pairs={{0,2},{1,3},{2,4},{3,5},{4,6},{5,7},{6,8},{7,9},{8,10},{9,11},{10,... | collective-permute-start | bytes 688136 | tf_op jit(solution)/shard_map/ppermute | solution.py:266
  417.0 9.4 %collective-permute-start.15 = (bf16[64,1792]{1,0:T(8,128)(2,1)S(1)}, bf16[64,1792]{1,0:T(8,128)(2,1)S(1)}, u32[]{:S(2)}, u32[]{:S(2)}) collective-permute-start(bf16[64,1792]{1,0:T(8,128)(2,1)S(1)} %shard_map.76), channel_id=1, source_target_pairs={{0,2},{1,3},{2,4},{3,5},{4,6},{5,7},{6,8},{7,9},{8,10},{9,11},{10,... | collective-permute-start | bytes 688136 | tf_op jit(solution)/shard_map/ppermute | solution.py:266
  420.9 10.7 %collective-permute-start.31 = (bf16[64,1792]{1,0:T(8,128)(2,1)S(1)}, bf16[64,1792]{1,0:T(8,128)(2,1)S(1)}, u32[]{:S(2)}, u32[]{:S(2)}) collective-permute-start(bf16[64,1792]{1,0:T(8,128)(2,1)S(1)} %shard_map.91), channel_id=1, source_target_pairs={{0,62},{1,63},{2,0},{3,1},{4,2},{5,3},{6,4},{7,5},{8,6},{9,7},{10,... | collective-permute-start | bytes 688136 | tf_op jit(solution)/shard_map/ppermute | solution.py:266
  (16 other events, 129.8 us)
